TPU v7x, 256 devices: a whole 4x4x8 slice. The times are simulated.
256 devices in a mesh: section: 8 (over z_lo, x), dp: 32 (over z_hi, y, core).
Axes of the slice: x: 4, y: 4, z: 8 (z_hi: 4, z_lo: 2; z = z_hi * 2 + z_lo), core: 2. Of those that a mesh axis runs over, the one named last changes fastest.
Arguments:
- activations: bfloat16 [8, 8, 1536, 5376], P('section', None, 'dp'), may hold values from -6 to 6
- loss_grads: bfloat16 [8, 1536, 5376], P(None, 'dp'), may hold values from -6 to 6
- adapter_in: bfloat16 [8, 5376, 64], P('section'), may hold values from -0.078125 to 0.078125
- adapter_out: bfloat16 [8, 64, 5376], P('section'), may hold values from -0.75 to 0.75
- first_moment: float32 [8, 32, 43008], P('section', 'dp'), may hold values from -0.4 to 0.4
- second_moment: float32 [8, 32, 43008], P('section', 'dp'), may hold values from 0.0001 to 0.01
- old_owner: int32 [8, 16], P('section'), may hold values from 0 to 31, as said below
- new_owner: int32 [8, 32], P('section'), may hold values from 0 to 31, each once within a row
- plan: int32 [8], replicated, may hold values from 0 to 7, each once
Outputs:
- input_grads: bfloat16 [8, 8, 1536, 5376], P('section', None, 'dp')
- adam_update: float32 [8, 32, 21504], P('section', 'dp')
- first_new: float32 [8, 32, 21504], P('section', 'dp')
- second_new: float32 [8, 32, 21504], P('section', 'dp')
Inputs may be any that keep to these rules, and one draw needn't show every extreme that they name: `old_owner`: the entries of one section's row are distinct.
All inputs are finite; a program needn't handle non-finite values.
Results may differ from a plain program's by a relative error of at most 0.025.
Values may be sent and summed in bfloat16 or wider, within the bound.
A program may use at most 64 MiB of HBM per device.

v0:
```python
import jax
import jax.numpy as jnp
from jax import lax
from jax.sharding import Mesh
from jax.sharding import PartitionSpec as P

DP = ("dp_0", "dp_1", "dp_2")


beta_one = 0.9
beta_two = 0.95
adam_eps = 1e-08
adam_step = 1000.0
loss_scale = 4096.0


def side_by_side(arrays, axis, split_dim, concat_dim, along):
    widths = [a.shape[along] for a in arrays]
    both = jnp.concatenate(arrays, axis=along)
    out = lax.all_to_all(both, axis, split_axis=split_dim, concat_axis=concat_dim, tiled=True)
    return tuple(jnp.split(out, [sum(widths[:k]) for k in range(1, len(widths))], axis=along))


def passed_along(value, axis, steps):
    count = lax.axis_size(axis)
    first, last = (max(0, -steps), min(count, count - steps))
    return lax.ppermute(value, axis, [(source, source + steps) for source in range(first, last)])


def cut_along(value, dim, size):
    before, after = (value.shape[:dim], value.shape[dim + 1 :])
    return jnp.moveaxis(value.reshape(*before, size, -1, *after), dim, 0)


def scatter_pairs(value, chips, core, dim):
    sizes = (lax.axis_size(chips), lax.axis_size(core))
    parts = cut_along(value, dim, sizes[0] * sizes[1])
    inside = parts.shape[1:]
    parts = parts.reshape(*sizes, *inside).swapaxes(0, 1).reshape(-1, *inside)
    parts = lax.psum_scatter(parts, core, scatter_dimension=0, tiled=True)
    return lax.psum_scatter(parts, chips, scatter_dimension=0, tiled=True)[0]


def silu_slope(pre_value):
    gate_value = jax.nn.sigmoid(pre_value)
    return gate_value * (1.0 + pre_value * (1.0 - gate_value))


def per_device(
    activations,
    loss_grads,
    adapter_in,
    adapter_out,
    first_moment,
    second_moment,
    old_owner,
    new_owner,
    plan,
):
    sections = lax.axis_size("section")
    section_index = lax.axis_index("section")
    replicas = lax.axis_size(DP)
    my_index = lax.axis_index(DP)
    weight_in = adapter_in[0]
    weight_out = adapter_out[0]
    inputs_all = activations[0]
    micro_count = inputs_all.shape[0]
    tok_rows = inputs_all.shape[1]
    width = inputs_all.shape[2]
    owners_old = old_owner[0]
    owners_new = new_owner[0]
    block_len = first_moment.shape[2] // 2
    replica_ids = jnp.arange(replicas, dtype=jnp.int32)
    new_block = jnp.sum(jnp.where(owners_new == my_index, replica_ids, 0))

    def drain_turn(turn_index, state):
        previous, grad_in, grad_out, emitted = state
        received = passed_along(previous, "section", -1)
        slot = turn_index - (sections - 1 - section_index)
        is_valid = (slot >= 0) & (slot < micro_count)
        clamped = jnp.clip(slot, 0, micro_count - 1)
        micro = lax.dynamic_index_in_dim(plan, clamped, 0, keepdims=False)
        section_input = lax.dynamic_index_in_dim(inputs_all, micro, 0, keepdims=False)
        from_loss = lax.dynamic_index_in_dim(loss_grads, micro, 0, keepdims=False)
        incoming = jnp.where(section_index == sections - 1, from_loss, received)
        pre_value = jnp.dot(section_input, weight_in, preferred_element_type=jnp.float32)
        hidden = jax.nn.silu(pre_value).astype(jnp.bfloat16)
        act_grad = jnp.dot(incoming, weight_out.T, preferred_element_type=jnp.float32)
        pre_grad = (act_grad * silu_slope(pre_value)).astype(jnp.bfloat16)
        input_grad = (
            incoming.astype(jnp.float32)
            + jnp.dot(pre_grad, weight_in.T, preferred_element_type=jnp.float32)
        ).astype(jnp.bfloat16)
        valid_weight = is_valid.astype(jnp.float32)
        grad_in = grad_in + valid_weight * jnp.dot(
            section_input.T, pre_grad, preferred_element_type=jnp.float32
        )
        grad_out = grad_out + valid_weight * jnp.dot(
            hidden.T, incoming, preferred_element_type=jnp.float32
        )
        earlier = lax.dynamic_index_in_dim(emitted, clamped, 0, keepdims=False)
        written = jnp.where(is_valid, input_grad, earlier)
        emitted = lax.dynamic_update_index_in_dim(emitted, written, clamped, 0)
        return (input_grad, grad_in, grad_out, emitted)

    start_state = (
        jnp.zeros((tok_rows, width), jnp.bfloat16),
        jnp.zeros(weight_in.shape, jnp.float32),
        jnp.zeros(weight_out.shape, jnp.float32),
        jnp.zeros((micro_count, tok_rows, width), jnp.bfloat16),
    )
    last_grad, grad_in, grad_out, emitted = lax.fori_loop(
        0, micro_count + sections - 1, drain_turn, start_state
    )
    partial_value = jnp.concatenate([grad_in.reshape(-1), grad_out.reshape(-1)])
    owner_match = owners_new[None, :] == replica_ids[:, None]
    inverse = jnp.sum(jnp.where(owner_match, replica_ids[None, :], 0), axis=1)
    ordered = jnp.take(partial_value.reshape(replicas, block_len), inverse, axis=0)
    grads = scatter_pairs(ordered, ("dp_0", "dp_1"), "dp_2", 0)[0] / loss_scale
    old_count = owners_old.shape[0]
    piece_len = 2 * block_len // replicas
    first_pieces = first_moment[0, 0].reshape(replicas, piece_len)
    second_pieces = second_moment[0, 0].reshape(replicas, piece_len)
    first_spread, second_spread = side_by_side((first_pieces, second_pieces), DP, 0, 0, 1)
    first_held = jnp.take(first_spread, owners_old, axis=0)
    second_held = jnp.take(second_spread, owners_old, axis=0)
    my_half = my_index // old_count
    targets = owners_new.reshape(-1, 2)
    target_of_block = jnp.where(my_half == 0, targets[:, 0], targets[:, 1])
    picker = (target_of_block[None, :] == replica_ids[:, None]).astype(jnp.float32)
    first_out = jnp.dot(picker, first_held, precision=lax.Precision.HIGHEST)
    second_out = jnp.dot(picker, second_held, precision=lax.Precision.HIGHEST)
    first_got = lax.all_to_all(first_out, DP, split_axis=0, concat_axis=0, tiled=True)
    second_got = lax.all_to_all(second_out, DP, split_axis=0, concat_axis=0, tiled=True)
    half_start = new_block % 2 * old_count
    first_mine = lax.dynamic_slice_in_dim(first_got, half_start, old_count, 0).reshape(-1)
    second_mine = lax.dynamic_slice_in_dim(second_got, half_start, old_count, 0).reshape(-1)
    moved = (first_mine, second_mine)
    first_old, second_old = moved
    first_next = beta_one * first_old + (1.0 - beta_one) * grads
    second_next = beta_two * second_old + (1.0 - beta_two) * grads * grads
    update = (
        first_next
        / (1.0 - beta_one**adam_step)
        / (jnp.sqrt(second_next / (1.0 - beta_two**adam_step)) + adam_eps)
    )
    return (emitted[None], update[None, None], first_next[None, None], second_next[None, None])


def solution(mesh):
    torus = Mesh(
        mesh.devices.reshape(mesh.shape["section"], 4, 4, 2), ("section", "dp_0", "dp_1", "dp_2")
    )
    in_specs = (
        P("section", None, DP, None),
        P(None, DP, None),
        P("section", None, None),
        P("section", None, None),
        P("section", DP, None),
        P("section", DP, None),
        P("section", None),
        P("section", None),
        P(),
    )
    out_specs = (
        P("section", None, DP, None),
        P("section", DP, None),
        P("section", DP, None),
        P("section", DP, None),
    )
    return jax.shard_map(
        per_device, mesh=torus, in_specs=in_specs, out_specs=out_specs, check_vma=False
    )
```

profile of v0, /device:TPU:6, one launch (start us, length us, event | category | flops | bytes accessed | tf_op | source)
XLA Modules:
  0.0 600.2 jit_solution(276154164992042437)
XLA Ops:
  12.1 340.5 %while.22 = (s32[]{:T(128)}, bf16[48,5376]{1,0:T(8,128)(2,1)}, f32[5376,64]{0,1:T(8,128)S(1)}, f32[64,5376]{1,0:T(8,128)}, bf16[8,48,5376]{2,1,0:T(8,128)(2,1)},...) while((s32[]{:T(128)}, bf16[48,5376]{1,0:T(8,128)(2,1)}, ...), condition=%wide.region_1.2_spmd.clone, body=%wide.region_0.1_spmd.clone.sunk | while | flops 168806416 | bytes 28440968 | solution.py:112
  20.9 9.9 %collective-permute-done = bf16[48,5376]{1,0:T(8,128)(2,1)} collective-permute-done((bf16[48,5376]{1,0:T(8,128)(2,1)}, bf16[48,5376]{1,0:T(8,128)(2,1)}, u32[]{:S(2)}, u32[]{:S(2)}) %collective-permute-start) | collective-permute-done | bytes 516128 | tf_op jit(solution)/shard_map/while/body/eval_jaxpr/ppermute | solution.py:27
  46.4 9.8 %collective-permute-done = bf16[48,5376]{1,0:T(8,128)(2,1)} collective-permute-done((bf16[48,5376]{1,0:T(8,128)(2,1)}, bf16[48,5376]{1,0:T(8,128)(2,1)}, u32[]{:S(2)}, u32[]{:S(2)}) %collective-permute-start) | collective-permute-done | bytes 516128 | tf_op jit(solution)/shard_map/while/body/eval_jaxpr/ppermute | solution.py:27
  71.8 9.0 %collective-permute-done = bf16[48,5376]{1,0:T(8,128)(2,1)} collective-permute-done((bf16[48,5376]{1,0:T(8,128)(2,1)}, bf16[48,5376]{1,0:T(8,128)(2,1)}, u32[]{:S(2)}, u32[]{:S(2)}) %collective-permute-start) | collective-permute-done | bytes 516128 | tf_op jit(solution)/shard_map/while/body/eval_jaxpr/ppermute | solution.py:27
  96.4 8.1 %collective-permute-done = bf16[48,5376]{1,0:T(8,128)(2,1)} collective-permute-done((bf16[48,5376]{1,0:T(8,128)(2,1)}, bf16[48,5376]{1,0:T(8,128)(2,1)}, u32[]{:S(2)}, u32[]{:S(2)}) %collective-permute-start) | collective-permute-done | bytes 516128 | tf_op jit(solution)/shard_map/while/body/eval_jaxpr/ppermute | solution.py:27
  120.1 7.3 %collective-permute-done = bf16[48,5376]{1,0:T(8,128)(2,1)} collective-permute-done((bf16[48,5376]{1,0:T(8,128)(2,1)}, bf16[48,5376]{1,0:T(8,128)(2,1)}, u32[]{:S(2)}, u32[]{:S(2)}) %collective-permute-start) | collective-permute-done | bytes 516128 | tf_op jit(solution)/shard_map/while/body/eval_jaxpr/ppermute | solution.py:27
  142.9 6.4 %collective-permute-done = bf16[48,5376]{1,0:T(8,128)(2,1)} collective-permute-done((bf16[48,5376]{1,0:T(8,128)(2,1)}, bf16[48,5376]{1,0:T(8,128)(2,1)}, u32[]{:S(2)}, u32[]{:S(2)}) %collective-permute-start) | collective-permute-done | bytes 516128 | tf_op jit(solution)/shard_map/while/body/eval_jaxpr/ppermute | solution.py:27
  164.9 6.3 %collective-permute-done = bf16[48,5376]{1,0:T(8,128)(2,1)} collective-permute-done((bf16[48,5376]{1,0:T(8,128)(2,1)}, bf16[48,5376]{1,0:T(8,128)(2,1)}, u32[]{:S(2)}, u32[]{:S(2)}) %collective-permute-start) | collective-permute-done | bytes 516128 | tf_op jit(solution)/shard_map/while/body/eval_jaxpr/ppermute | solution.py:27
  186.8 6.3 %collective-permute-done = bf16[48,5376]{1,0:T(8,128)(2,1)} collective-permute-done((bf16[48,5376]{1,0:T(8,128)(2,1)}, bf16[48,5376]{1,0:T(8,128)(2,1)}, u32[]{:S(2)}, u32[]{:S(2)}) %collective-permute-start) | collective-permute-done | bytes 516128 | tf_op jit(solution)/shard_map/while/body/eval_jaxpr/ppermute | solution.py:27
  208.6 6.3 %collective-permute-done = bf16[48,5376]{1,0:T(8,128)(2,1)} collective-permute-done((bf16[48,5376]{1,0:T(8,128)(2,1)}, bf16[48,5376]{1,0:T(8,128)(2,1)}, u32[]{:S(2)}, u32[]{:S(2)}) %collective-permute-start) | collective-permute-done | bytes 516128 | tf_op jit(solution)/shard_map/while/body/eval_jaxpr/ppermute | solution.py:27
  230.5 6.3 %collective-permute-done = bf16[48,5376]{1,0:T(8,128)(2,1)} collective-permute-done((bf16[48,5376]{1,0:T(8,128)(2,1)}, bf16[48,5376]{1,0:T(8,128)(2,1)}, u32[]{:S(2)}, u32[]{:S(2)}) %collective-permute-start) | collective-permute-done | bytes 516128 | tf_op jit(solution)/shard_map/while/body/eval_jaxpr/ppermute | solution.py:27
  252.3 6.3 %collective-permute-done = bf16[48,5376]{1,0:T(8,128)(2,1)} collective-permute-done((bf16[48,5376]{1,0:T(8,128)(2,1)}, bf16[48,5376]{1,0:T(8,128)(2,1)}, u32[]{:S(2)}, u32[]{:S(2)}) %collective-permute-start) | collective-permute-done | bytes 516128 | tf_op jit(solution)/shard_map/while/body/eval_jaxpr/ppermute | solution.py:27
  274.2 6.3 %collective-permute-done = bf16[48,5376]{1,0:T(8,128)(2,1)} collective-permute-done((bf16[48,5376]{1,0:T(8,128)(2,1)}, bf16[48,5376]{1,0:T(8,128)(2,1)}, u32[]{:S(2)}, u32[]{:S(2)}) %collective-permute-start) | collective-permute-done | bytes 516128 | tf_op jit(solution)/shard_map/while/body/eval_jaxpr/ppermute | solution.py:27
  296.0 6.3 %collective-permute-done = bf16[48,5376]{1,0:T(8,128)(2,1)} collective-permute-done((bf16[48,5376]{1,0:T(8,128)(2,1)}, bf16[48,5376]{1,0:T(8,128)(2,1)}, u32[]{:S(2)}, u32[]{:S(2)}) %collective-permute-start) | collective-permute-done | bytes 516128 | tf_op jit(solution)/shard_map/while/body/eval_jaxpr/ppermute | solution.py:27
  317.9 6.3 %collective-permute-done = bf16[48,5376]{1,0:T(8,128)(2,1)} collective-permute-done((bf16[48,5376]{1,0:T(8,128)(2,1)}, bf16[48,5376]{1,0:T(8,128)(2,1)}, u32[]{:S(2)}, u32[]{:S(2)}) %collective-permute-start) | collective-permute-done | bytes 516128 | tf_op jit(solution)/shard_map/while/body/eval_jaxpr/ppermute | solution.py:27
  339.7 6.3 %collective-permute-done = bf16[48,5376]{1,0:T(8,128)(2,1)} collective-permute-done((bf16[48,5376]{1,0:T(8,128)(2,1)}, bf16[48,5376]{1,0:T(8,128)(2,1)}, u32[]{:S(2)}, u32[]{:S(2)}) %collective-permute-start) | collective-permute-done | bytes 516128 | tf_op jit(solution)/shard_map/while/body/eval_jaxpr/ppermute | solution.py:27
  370.1 4.4 copy.27
  378.9 11.3 %all-to-all-start = ((f32[32,1,2688]{2,1,0:T(1,128)}), f32[32,1,2688]{2,1,0:T(1,128)S(1)}, u32[]{:S(2)}, u32[]{:S(2)}) async-start(f32[32,1,2688]{2,1,0:T(1,128)} %all_to_all.20), calls=%async_computation | async-start | bytes 688128 | tf_op jit(solution)/shard_map/all_to_all | solution.py:20
  393.1 17.5 %all-reduce.5.cloned.1.call-done = f32[32,1,21504]{2,1,0:T(1,128)} async-done(((f32[32,1,21504]{2,1,0:T(1,128)}), f32[32,1,21504]{2,1,0:T(1,128)}) %all-reduce.5.cloned.1.call-update) | async-done | bytes 2752528
  415.0 9.9 %all-to-all-start.2 = ((f32[32,1,1344]{2,1,0:T(1,128)}), f32[32,1,1344]{2,1,0:T(1,128)S(1)}, u32[]{:S(2)}, u32[]{:S(2)}) async-start(f32[32,1,1344]{2,1,0:T(1,128)} %copy.28), calls=%async_computation.2 | async-start | bytes 360448 | tf_op jit(solution)/shard_map/all_to_all | solution.py:134
  426.6 11.0 %all-to-all-done.2 = f32[32,1,1344]{2,1,0:T(1,128)S(1)} async-done(((f32[32,1,1344]{2,1,0:T(1,128)}), f32[32,1,1344]{2,1,0:T(1,128)S(1)}, u32[]{:S(2)}, u32[]{:S(2)}) %all-to-all-start.2) | async-done | bytes 172064 | tf_op jit(solution)/shard_map/all_to_all | solution.py:134
  437.7 4.3 all-to-all-start.1
  445.5 8.8 %all-to-all-done.1 = f32[32,1,1344]{2,1,0:T(1,128)S(1)} async-done(((f32[32,1,1344]{2,1,0:T(1,128)}), f32[32,1,1344]{2,1,0:T(1,128)S(1)}, u32[]{:S(2)}, u32[]{:S(2)}) %all-to-all-start.1) | async-done | bytes 172064 | tf_op jit(solution)/shard_map/all_to_all | solution.py:133
  454.8 136.1 %all-reduce.7.cloned.1.call-done = f32[16,1,21504]{2,1,0:T(1,128)} async-done(((f32[16,1,21504]{2,1,0:T(1,128)}), f32[16,1,21504]{2,1,0:T(1,128)}) %all-reduce.7.cloned.1.call-update) | async-done | bytes 1376272
  (279 shorter events, 241.1 us)
Async XLA Ops:
  7.2 403.4 %all-reduce.5.cloned.1.call-start = ((), (), s32[]{:S(2)}) async-start(), calls=%async_computation.3 | async-start | bytes 5505024
  13.0 17.8 %collective-permute-start = (bf16[48,5376]{1,0:T(8,128)(2,1)}, bf16[48,5376]{1,0:T(8,128)(2,1)}, u32[]{:S(2)}, u32[]{:S(2)}) collective-permute-start(bf16[48,5376]{1,0:T(8,128)(2,1)} %broadcast_select_fusion.2), channel_id=1, source_target_pairs={{32,0},{64,32},{96,64},{128,96},{160,128},{192,160},{224,192},{33,... | collective-permute-start | bytes 1548296 | tf_op jit(solution)/shard_map/while/body/eval_jaxpr/ppermute | solution.py:27
  39.2 17.0 %collective-permute-start = (bf16[48,5376]{1,0:T(8,128)(2,1)}, bf16[48,5376]{1,0:T(8,128)(2,1)}, u32[]{:S(2)}, u32[]{:S(2)}) collective-permute-start(bf16[48,5376]{1,0:T(8,128)(2,1)} %broadcast_select_fusion.2), channel_id=1, source_target_pairs={{32,0},{64,32},{96,64},{128,96},{160,128},{192,160},{224,192},{33,... | collective-permute-start | bytes 1548296 | tf_op jit(solution)/shard_map/while/body/eval_jaxpr/ppermute | solution.py:27
  64.7 16.1 %collective-permute-start = (bf16[48,5376]{1,0:T(8,128)(2,1)}, bf16[48,5376]{1,0:T(8,128)(2,1)}, u32[]{:S(2)}, u32[]{:S(2)}) collective-permute-start(bf16[48,5376]{1,0:T(8,128)(2,1)} %broadcast_select_fusion.2), channel_id=1, source_target_pairs={{32,0},{64,32},{96,64},{128,96},{160,128},{192,160},{224,192},{33,... | collective-permute-start | bytes 1548296 | tf_op jit(solution)/shard_map/while/body/eval_jaxpr/ppermute | solution.py:27
  89.2 15.2 %collective-permute-start = (bf16[48,5376]{1,0:T(8,128)(2,1)}, bf16[48,5376]{1,0:T(8,128)(2,1)}, u32[]{:S(2)}, u32[]{:S(2)}) collective-permute-start(bf16[48,5376]{1,0:T(8,128)(2,1)} %broadcast_select_fusion.2), channel_id=1, source_target_pairs={{32,0},{64,32},{96,64},{128,96},{160,128},{192,160},{224,192},{33,... | collective-permute-start | bytes 1548296 | tf_op jit(solution)/shard_map/while/body/eval_jaxpr/ppermute | solution.py:27
  113.0 14.4 %collective-permute-start = (bf16[48,5376]{1,0:T(8,128)(2,1)}, bf16[48,5376]{1,0:T(8,128)(2,1)}, u32[]{:S(2)}, u32[]{:S(2)}) collective-permute-start(bf16[48,5376]{1,0:T(8,128)(2,1)} %broadcast_select_fusion.2), channel_id=1, source_target_pairs={{32,0},{64,32},{96,64},{128,96},{160,128},{192,160},{224,192},{33,... | collective-permute-start | bytes 1548296 | tf_op jit(solution)/shard_map/while/body/eval_jaxpr/ppermute | solution.py:27
  135.8 13.5 %collective-permute-start = (bf16[48,5376]{1,0:T(8,128)(2,1)}, bf16[48,5376]{1,0:T(8,128)(2,1)}, u32[]{:S(2)}, u32[]{:S(2)}) collective-permute-start(bf16[48,5376]{1,0:T(8,128)(2,1)} %broadcast_select_fusion.2), channel_id=1, source_target_pairs={{32,0},{64,32},{96,64},{128,96},{160,128},{192,160},{224,192},{33,... | collective-permute-start | bytes 1548296 | tf_op jit(solution)/shard_map/while/body/eval_jaxpr/ppermute | solution.py:27
  157.8 13.4 %collective-permute-start = (bf16[48,5376]{1,0:T(8,128)(2,1)}, bf16[48,5376]{1,0:T(8,128)(2,1)}, u32[]{:S(2)}, u32[]{:S(2)}) collective-permute-start(bf16[48,5376]{1,0:T(8,128)(2,1)} %broadcast_select_fusion.2), channel_id=1, source_target_pairs={{32,0},{64,32},{96,64},{128,96},{160,128},{192,160},{224,192},{33,... | collective-permute-start | bytes 1548296 | tf_op jit(solution)/shard_map/while/body/eval_jaxpr/ppermute | solution.py:27
  179.7 13.4 %collective-permute-start = (bf16[48,5376]{1,0:T(8,128)(2,1)}, bf16[48,5376]{1,0:T(8,128)(2,1)}, u32[]{:S(2)}, u32[]{:S(2)}) collective-permute-start(bf16[48,5376]{1,0:T(8,128)(2,1)} %broadcast_select_fusion.2), channel_id=1, source_target_pairs={{32,0},{64,32},{96,64},{128,96},{160,128},{192,160},{224,192},{33,... | collective-permute-start | bytes 1548296 | tf_op jit(solution)/shard_map/while/body/eval_jaxpr/ppermute | solution.py:27
  201.5 13.4 %collective-permute-start = (bf16[48,5376]{1,0:T(8,128)(2,1)}, bf16[48,5376]{1,0:T(8,128)(2,1)}, u32[]{:S(2)}, u32[]{:S(2)}) collective-permute-start(bf16[48,5376]{1,0:T(8,128)(2,1)} %broadcast_select_fusion.2), channel_id=1, source_target_pairs={{32,0},{64,32},{96,64},{128,96},{160,128},{192,160},{224,192},{33,... | collective-permute-start | bytes 1548296 | tf_op jit(solution)/shard_map/while/body/eval_jaxpr/ppermute | solution.py:27
  223.4 13.4 %collective-permute-start = (bf16[48,5376]{1,0:T(8,128)(2,1)}, bf16[48,5376]{1,0:T(8,128)(2,1)}, u32[]{:S(2)}, u32[]{:S(2)}) collective-permute-start(bf16[48,5376]{1,0:T(8,128)(2,1)} %broadcast_select_fusion.2), channel_id=1, source_target_pairs={{32,0},{64,32},{96,64},{128,96},{160,128},{192,160},{224,192},{33,... | collective-permute-start | bytes 1548296 | tf_op jit(solution)/shard_map/while/body/eval_jaxpr/ppermute | solution.py:27
  245.2 13.4 %collective-permute-start = (bf16[48,5376]{1,0:T(8,128)(2,1)}, bf16[48,5376]{1,0:T(8,128)(2,1)}, u32[]{:S(2)}, u32[]{:S(2)}) collective-permute-start(bf16[48,5376]{1,0:T(8,128)(2,1)} %broadcast_select_fusion.2), channel_id=1, source_target_pairs={{32,0},{64,32},{96,64},{128,96},{160,128},{192,160},{224,192},{33,... | collective-permute-start | bytes 1548296 | tf_op jit(solution)/shard_map/while/body/eval_jaxpr/ppermute | solution.py:27
  267.1 13.4 %collective-permute-start = (bf16[48,5376]{1,0:T(8,128)(2,1)}, bf16[48,5376]{1,0:T(8,128)(2,1)}, u32[]{:S(2)}, u32[]{:S(2)}) collective-permute-start(bf16[48,5376]{1,0:T(8,128)(2,1)} %broadcast_select_fusion.2), channel_id=1, source_target_pairs={{32,0},{64,32},{96,64},{128,96},{160,128},{192,160},{224,192},{33,... | collective-permute-start | bytes 1548296 | tf_op jit(solution)/shard_map/while/body/eval_jaxpr/ppermute | solution.py:27
  288.9 13.4 %collective-permute-start = (bf16[48,5376]{1,0:T(8,128)(2,1)}, bf16[48,5376]{1,0:T(8,128)(2,1)}, u32[]{:S(2)}, u32[]{:S(2)}) collective-permute-start(bf16[48,5376]{1,0:T(8,128)(2,1)} %broadcast_select_fusion.2), channel_id=1, source_target_pairs={{32,0},{64,32},{96,64},{128,96},{160,128},{192,160},{224,192},{33,... | collective-permute-start | bytes 1548296 | tf_op jit(solution)/shard_map/while/body/eval_jaxpr/ppermute | solution.py:27
  310.8 13.4 %collective-permute-start = (bf16[48,5376]{1,0:T(8,128)(2,1)}, bf16[48,5376]{1,0:T(8,128)(2,1)}, u32[]{:S(2)}, u32[]{:S(2)}) collective-permute-start(bf16[48,5376]{1,0:T(8,128)(2,1)} %broadcast_select_fusion.2), channel_id=1, source_target_pairs={{32,0},{64,32},{96,64},{128,96},{160,128},{192,160},{224,192},{33,... | collective-permute-start | bytes 1548296 | tf_op jit(solution)/shard_map/while/body/eval_jaxpr/ppermute | solution.py:27
  332.6 13.4 %collective-permute-start = (bf16[48,5376]{1,0:T(8,128)(2,1)}, bf16[48,5376]{1,0:T(8,128)(2,1)}, u32[]{:S(2)}, u32[]{:S(2)}) collective-permute-start(bf16[48,5376]{1,0:T(8,128)(2,1)} %broadcast_select_fusion.2), channel_id=1, source_target_pairs={{32,0},{64,32},{96,64},{128,96},{160,128},{192,160},{224,192},{33,... | collective-permute-start | bytes 1548296 | tf_op jit(solution)/shard_map/while/body/eval_jaxpr/ppermute | solution.py:27
  376.6 14.2 %copy-start.7 = (s32[1,32]{1,0:T(1,128)S(1)}, s32[1,32]{1,0:T(1,128)}, u32[]{:S(2)}) copy-start(s32[1,32]{1,0:T(1,128)} %param.20) | copy-start | bytes 388
  376.6 15.0 %copy-start.9 = (u32[256]{0:T(256)S(1)}, u32[256]{0:T(256)}, u32[]{:S(2)}) copy-start(u32[256]{0:T(256)} %constant.175) | copy-start | bytes 3076
  376.6 16.4 %copy-start.6 = (s32[1,16]{1,0:T(1,128)S(1)}, s32[1,16]{1,0:T(1,128)}, u32[]{:S(2)}) copy-start(s32[1,16]{1,0:T(1,128)} %param.19) | copy-start | bytes 196
  378.9 34.2 %all-to-all-start = ((f32[32,1,2688]{2,1,0:T(1,128)}), f32[32,1,2688]{2,1,0:T(1,128)S(1)}, u32[]{:S(2)}, u32[]{:S(2)}) async-start(f32[32,1,2688]{2,1,0:T(1,128)} %all_to_all.20), calls=%async_computation | async-start | bytes 688128 | tf_op jit(solution)/shard_map/all_to_all | solution.py:20
  390.3 200.5 %all-reduce.7.cloned.1.call-start = ((), (), s32[]{:S(2)}) async-start(), calls=%async_computation.4 | async-start | bytes 2752512
  413.8 30.7 %copy-start.8 = (u32[256]{0:T(256)S(1)}, u32[256]{0:T(256)}, u32[]{:S(2)}) copy-start(u32[256]{0:T(256)} %constant.179) | copy-start | bytes 3076
  415.0 22.7 %all-to-all-start.2 = ((f32[32,1,1344]{2,1,0:T(1,128)}), f32[32,1,1344]{2,1,0:T(1,128)S(1)}, u32[]{:S(2)}, u32[]{:S(2)}) async-start(f32[32,1,1344]{2,1,0:T(1,128)} %copy.28), calls=%async_computation.2 | async-start | bytes 360448 | tf_op jit(solution)/shard_map/all_to_all | solution.py:134
  437.7 16.7 %all-to-all-start.1 = ((f32[32,1,1344]{2,1,0:T(1,128)}), f32[32,1,1344]{2,1,0:T(1,128)S(1)}, u32[]{:S(2)}, u32[]{:S(2)}) async-start(f32[32,1,1344]{2,1,0:T(1,128)} %copy.25), calls=%async_computation.1 | async-start | bytes 360448 | tf_op jit(solution)/shard_map/all_to_all | solution.py:133
  (34 other events, 50.0 us)
Sparse Core Ops, SparseCore 0:
  374.7 35.8 all-reduce.4
  413.2 177.5 all-reduce.6
where the time goes:
time: 605 us; the launch traced here: 600 us
  waiting for transfers between devices  281 us (46%)
  matrix products  84.5 us (14%)
  local copies, waits for them, and re-layouts  74.6 us (12%)
  other arithmetic  56.8 us (9%)
  starting transfers between devices  55 us (9%)
  loops' own time  31.7 us (5%)
  between operations  17 us (3%)
    unnamed x4, waiting for transfers between devices  154 us
    ppermute x15, waiting for transfers between devices, passed_along(): lax.ppermute(value, axis, [(source, source + steps) for source in range(f...  107 us
    another operation x1, loops' own time, per_device(): lax.fori_loop(0, micro_count + sections - 1, drain_turn, start_state)  31.7 us
    ppermute x15, starting transfers between devices, passed_along(): lax.ppermute(value, axis, [(source, source + steps) for source in range(f...  29.5 us
    while x15, other arithmetic  27.3 us
    dot_general x15, matrix products, drain_turn(): jnp.dot(section_input.T, pre_grad, preferred_element_type=jnp.float32)  26.1 us
    dot_general x15, matrix products, drain_turn(): jnp.dot(pre_grad, weight_in.T, preferred_element_type=jnp.float32)  23.8 us
    dot_general x15, matrix products, drain_turn(): jnp.dot(section_input, weight_in, preferred_element_type=jnp.float32)  21 us
  transfers between devices with their start and end apart: 20, of which 19 were waited for; matrix products, arithmetic and copies ran while one was open for 10% of the time, Pallas kernels for 0%

commit v1 on v0

v1 whole, which is shorter than its diff:
```python
import functools

import jax
import jax.numpy as jnp
from jax import lax
from jax.experimental import pallas as pl
from jax.experimental.pallas import tpu as pltpu
from jax.sharding import Mesh
from jax.sharding import PartitionSpec as P

DP = ("dp_0", "dp_1", "dp_2")
ND, NY, NC = 4, 4, 2
SECTIONS = 8
RELAYS = 7
ALONG_Z = (1, 3, 5)
MESH = pl.DeviceIdType.MESH
BF = jnp.bfloat16
F32 = jnp.float32

beta_one = 0.9
beta_two = 0.95
adam_eps = 1e-08
adam_step = 1000.0
loss_scale = 4096.0


def dp_coords(index):
    return {"dp_0": index // (NY * NC), "dp_1": lax.rem(index // NC, NY), "dp_2": lax.rem(index, NC)}


def relay_spot(index):
    return 4 * index + index % 4


def drain_kernel(
    table_ref,
    inputs_ref,
    base_ref,
    turned_ref,
    rows_ref,
    weight_in_ref,
    weight_out_ref,
    first_ref,
    second_ref,
    p_ref,
    moved_ref,
    whole_ref,
    sum_ref,
    inputs,
    base,
    pre_sum,
    act_sum,
    hidden,
    rows_got,
    packed,
    prod,
    uv_out,
    uv_got,
    total,
    spread,
    picked,
    grad,
    flat,
    mixed_rows,
    held,
    half_out,
    half_got,
    y_out,
    y_got,
    z_out,
    z_got,
    load_sem,
    rows_send,
    rows_recv,
    prod_send,
    prod_recv,
    uv_send,
    uv_recv,
    gather_send,
    gather_recv,
    p_send,
    p_recv,
    spread_send,
    spread_recv,
    moved_send,
    moved_recv,
    slice_send,
    slice_recv,
    wide_send,
    wide_recv,
    pair_send,
    pair_recv,
    half_send,
    half_recv,
    y_send,
    y_recv,
    z_send,
    z_recv,
):
    sections = SECTIONS
    replicas = ND * NY * NC
    me = lax.axis_index("section")
    z = lax.axis_index("dp_0")
    y = lax.axis_index("dp_1")
    core = lax.axis_index("dp_2")
    dp = (z * NY + y) * NC + core
    other = 1 - core
    tokens, width = inputs.shape
    rank = weight_in_ref.shape[0]
    tok_rows = tokens // sections
    lanes = sections * rank
    parts = load_sem.shape[1]
    chunk = width // parts
    groups = chunk // 128
    block_rows = flat.shape[0] // (replicas // 2)
    half_blocks = replicas // 2
    extra = held.shape[1] - block_rows

    def load(which, part):
        source, target = ((inputs_ref, inputs), (base_ref, base))[which]
        columns = pl.ds(pl.multiple_of(part * chunk, 128), chunk)
        return pltpu.make_async_copy(
            source.at[:, columns], target.at[:, columns], load_sem.at[which, part]
        )

    for part in range(parts):
        load(0, part).start()
        load(1, part).start()

    barrier = pltpu.get_barrier_semaphore()
    for step in range(1, sections):
        pl.semaphore_signal(
            barrier, inc=1, device_id={"section": lax.rem(me + step, sections)}, device_id_type=MESH
        )

    def greet(step, carry):
        pl.semaphore_signal(
            barrier, inc=1, device_id=dp_coords(lax.rem(dp + step, replicas)), device_id_type=MESH
        )
        return carry

    lax.fori_loop(1, replicas, greet, 0)
    pl.semaphore_wait(barrier, sections - 1 + replicas - 1)

    def section_copy(src, dst, send, recv, target):
        return pltpu.make_async_remote_copy(
            src_ref=src,
            dst_ref=dst,
            send_sem=send,
            recv_sem=recv,
            device_id={"section": target},
            device_id_type=MESH,
        )

    def took(view, sem):
        section_copy(view, view, sem, sem, me).wait_recv()

    def sent(view, sem):
        section_copy(view, view, sem, sem, me).wait_send()

    hop = dp // 4

    def rows_copy():
        return section_copy(
            rows_ref.at[:, lax.rem(dp, 4)],
            rows_got,
            rows_send,
            rows_recv,
            lax.rem(me + sections - hop, sections),
        )

    @pl.when(me < hop)
    def _():
        rows_copy().start()

    def along_z(section):
        return lax.rem(section, 2) * (1 - section // 7)

    def row_of(section):
        return y + along_z(section) * (z - y)

    for section in range(1, sections):

        @pl.when(me == section)
        def _(section=section):
            row = z if section in ALONG_Z else y
            for target in reversed(range(section)):
                section_copy(
                    turned_ref.at[row, core],
                    whole_ref.at[section, row, core],
                    slice_send,
                    slice_recv.at[section],
                    target,
                ).start()

    relay = dp // 4
    is_relay = (lax.rem(dp, 4) == lax.rem(relay, 4)) & (relay < RELAYS)

    def spread_copy(which, index):
        source = first_ref if which == 0 else second_ref
        peer = relay_spot(index)
        return pltpu.make_async_remote_copy(
            src_ref=source.at[:, index],
            dst_ref=spread.at[dp, which],
            send_sem=spread_send,
            recv_sem=spread_recv,
            device_id={"dp_0": peer // 8, "dp_1": peer // 2 % 4, "dp_2": peer % 2},
            device_id_type=MESH,
        )

    for index in range(RELAYS):

        @pl.when(dp != relay_spot(index))
        def _(index=index):
            spread_copy(0, index).start()
            spread_copy(1, index).start()

        @pl.when(dp == relay_spot(index))
        def _(index=index):
            spread[relay_spot(index), 0] = first_ref[:, index]
            spread[relay_spot(index), 1] = second_ref[:, index]

    across = (((1,), (1,)), ((), ()))
    down = (((0,), (0,)), ((), ()))
    pre_sum[...] = jnp.zeros_like(pre_sum)
    act_sum[...] = jnp.zeros_like(act_sum)

    def accumulate(part, carry):
        columns = pl.ds(pl.multiple_of(part * chunk, 128), chunk)
        load(0, part).wait()
        pre_sum[...] += lax.dot_general(
            inputs[:, columns], weight_in_ref[:, columns], across, preferred_element_type=F32
        )
        load(1, part).wait()
        act_sum[...] += lax.dot_general(
            base[:, columns], weight_out_ref[:, columns], across, preferred_element_type=F32
        )
        return carry

    lax.fori_loop(0, parts, accumulate, 0)
    pre_value = pre_sum[...]
    gate = jax.nn.sigmoid(pre_value)
    hidden[...] = (pre_value * gate).astype(BF)
    slope = gate * (1.0 + pre_value * (1.0 - gate))
    both = jnp.concatenate([act_sum[...].astype(BF), slope.astype(BF)], axis=1)
    uv_out[...] = both.reshape(sections, tok_rows, 2 * rank)

    def uv_copy(step):
        target = lax.rem(me + step, sections)
        return section_copy(uv_out.at[target], uv_got.at[me], uv_send, uv_recv, target)

    for step in range(1, sections):
        uv_copy(step).start()
    uv_got[me] = uv_out[me]

    slot = lax.rem(hop + me, sections) * 4 + lax.rem(dp, 4)
    valid = me + hop >= sections

    def prod_copy(step):
        return pltpu.make_async_remote_copy(
            src_ref=packed,
            dst_ref=prod.at[me, slot],
            send_sem=prod_send,
            recv_sem=prod_recv,
            device_id=dp_coords(lax.rem(dp + step, replicas)),
            device_id_type=MESH,
        )

    @pl.when(valid)
    def _():
        took(rows_got, rows_recv)
        pieces = [
            lax.dot_general(rows_got[k], weight_in_ref[...], across, preferred_element_type=F32)
            for k in range(2)
        ]
        packed[...] = jnp.concatenate(pieces, axis=1).astype(BF)

        def prod_start(step, carry):
            prod_copy(step).start()
            return carry

        lax.fori_loop(1, replicas, prod_start, 0)
        prod[me, slot] = packed[...]

    def outward(part, carry):
        columns = pl.ds(pl.multiple_of(part * chunk, 128), chunk)
        result = lax.dot_general(hidden[...], base[:, columns], down, preferred_element_type=F32)
        for group in range(groups):
            flat[pl.ds(part * groups + group, rank, stride=width // 128), :] = result[
                :, group * 128 : (group + 1) * 128
            ]
        return carry

    lax.fori_loop(0, parts, outward, 0)
    for block in range(half_blocks):
        held[half_blocks + block, :block_rows] = flat[pl.ds(block * block_rows, block_rows), :]

    for section in range(1, sections):

        @pl.when((me == section) & valid)
        def _(section=section):
            took(prod.at[0, pl.ds(0, 4 * section - 1)], prod_recv)

        @pl.when((me == section) & (me + hop < sections))
        def _(section=section):
            took(prod.at[0, pl.ds(0, 4 * section)], prod_recv)

        @pl.when(me == section)
        def _(section=section):
            for step in range(1, sections):
                section_copy(
                    prod.at[section, pl.ds(0, 4 * section)],
                    prod.at[section, pl.ds(0, 4 * section)],
                    gather_send,
                    gather_recv.at[section],
                    (section - step) % sections,
                ).start()

    def wide_copy(section, shift):
        view = whole_ref.at[section, row_of(section), core]
        axis, at, count = ("dp_0", z, ND) if section in ALONG_Z else ("dp_1", y, NY)
        return pltpu.make_async_remote_copy(
            src_ref=view,
            dst_ref=view,
            send_sem=wide_send.at[section],
            recv_sem=wide_recv.at[section],
            device_id={axis: lax.rem(at + shift, count)},
            device_id_type=MESH,
        )

    for section in range(1, sections):

        @pl.when(me < section)
        def _(section=section):
            took(whole_ref.at[section, row_of(section), core], slice_recv.at[section])
            for shift in (1, 3, 2):
                wide_copy(section, shift).start()

    def moved_copy(step):
        peer = lax.rem(dp + step, replicas)
        return pltpu.make_async_remote_copy(
            src_ref=picked.at[peer],
            dst_ref=moved_ref.at[:, relay],
            send_sem=moved_send,
            recv_sem=moved_recv,
            device_id=dp_coords(peer),
            device_id_type=MESH,
        )

    @pl.when(is_relay)
    def _():
        took(spread.at[pl.ds(0, replicas - 1)], spread_recv)

        def pick(target, carry):
            owner = table_ref[0, target]
            half = table_ref[1, target]
            picked[target, 0] = spread[owner, 0, half]
            picked[target, 1] = spread[owner, 1, half]
            return carry

        lax.fori_loop(0, replicas, pick, 0)

        def moved_start(step, carry):
            moved_copy(step).start()
            return carry

        lax.fori_loop(1, replicas, moved_start, 0)
        moved_ref[:, relay] = picked[dp]

    took(uv_got.at[pl.ds(0, sections - 1)], uv_recv)
    for section in range(1, sections):

        @pl.when(me != section)
        def _(section=section):
            took(prod.at[section, pl.ds(0, 4 * section)], gather_recv.at[section])

    total[...] = jnp.zeros_like(total)
    for turn in reversed(range(sections)):
        low, high = turn * rank, (turn + 1) * rank
        pair = uv_got[turn].astype(F32)
        p_value = ((pair[:, :rank] + total[:, low:high]) * pair[:, rank:]).astype(BF)
        p_ref[me, :, low:high] = p_value
        if turn:
            got = prod[turn, : 4 * turn].astype(F32).reshape(turn, 32, 2 * rank)
            rows = jnp.concatenate([got[:, :, :rank], got[:, :, rank:]], axis=1)
            rows = rows.reshape(turn * rank, rank).astype(BF)
            total[:, :low] += lax.dot_general(p_value, rows, across, preferred_element_type=F32)

    def live(section):
        start = section // 2 * 2 * rank
        return pl.ds(start, lanes - start)

    def p_copy(section):
        view = p_ref.at[me, :, live(section)]
        return section_copy(view, view, p_send.at[section], p_recv, section)

    for section in range(sections):

        @pl.when(me != section)
        def _(section=section):
            p_copy(section).start()

    for section in range(sections):

        @pl.when(me == section)
        def _(section=section):
            took(p_ref.at[pl.ds(0, sections - 1), :, live(section)], p_recv)

    lane_section = lax.broadcasted_iota(jnp.int32, (tokens, lanes), 1) // rank
    p_all = p_ref[...].reshape(tokens, lanes)
    p_above = jnp.where(lane_section > me, p_all, jnp.zeros_like(p_all))
    p_live = jnp.where(lane_section == me, p_all, jnp.zeros_like(p_all))
    take = lax.rem(lax.broadcasted_iota(jnp.int32, (lanes, rank), 0), rank) == (
        lax.broadcasted_iota(jnp.int32, (lanes, rank), 1)
    )
    p_mine = jnp.dot(p_live, take.astype(F32).astype(BF), preferred_element_type=F32).astype(BF)

    def inward(part, carry):
        columns = pl.ds(pl.multiple_of(part * chunk, 128), chunk)
        grad[columns, :] = lax.dot_general(
            inputs[:, columns], p_mine, down, preferred_element_type=F32
        )
        return carry

    lax.fori_loop(0, parts, inward, 0)
    mixed = lax.dot_general(hidden[...], p_above, down, preferred_element_type=F32)
    for group in range(lanes // 128):
        mixed_rows[pl.ds(group, rank, stride=lanes // 128), :] = mixed[
            :, group * 128 : (group + 1) * 128
        ]
    for block in range(half_blocks):
        even = grad[pl.ds(block * 2 * block_rows, block_rows, stride=2), :]
        odd = grad[pl.ds(block * 2 * block_rows + 1, block_rows, stride=2), :]
        held[block, :block_rows] = jnp.concatenate([even, odd], axis=1)
        held[block, block_rows:] = jnp.zeros((extra, 128), F32)
        held[half_blocks + block, block_rows:] = mixed_rows[pl.ds(block * extra, extra), :]

    order = (2, 1, 3, 0)

    def half_copy(far):
        return pltpu.make_async_remote_copy(
            src_ref=half_out.at[far],
            dst_ref=half_got.at[far],
            send_sem=half_send.at[far],
            recv_sem=half_recv.at[far],
            device_id={"dp_2": other},
            device_id_type=MESH,
        )

    def y_copy(far, step):
        there = lax.rem(y + step, NY)
        return pltpu.make_async_remote_copy(
            src_ref=y_out.at[far, there],
            dst_ref=y_got.at[far, step],
            send_sem=y_send.at[far],
            recv_sem=y_recv.at[far],
            device_id={"dp_1": there},
            device_id_type=MESH,
        )

    def z_copy(far):
        return pltpu.make_async_remote_copy(
            src_ref=z_out.at[far],
            dst_ref=z_got.at[far],
            send_sem=z_send.at[far],
            recv_sem=z_recv.at[far],
            device_id={"dp_0": lax.rem(z + far, ND)},
            device_id_type=MESH,
        )

    for far in order:
        there = lax.rem(z + far, ND)
        for column in range(NY):
            half_out[far, column] = held[table_ref[2, (other * ND + there) * NY + column]].astype(BF)
        half_copy(far).start()
    for far in order:
        there = lax.rem(z + far, ND)
        half_copy(far).wait_recv()
        for column in range(NY):
            own = held[table_ref[2, (core * ND + there) * NY + column]]
            y_out[far, column] = (own + half_got[far, column].astype(F32)).astype(BF)
        for step in (2, 1, 3):
            y_copy(far, step).start()
    for far in order:
        took(y_got.at[far, pl.ds(1, NY - 1)], y_recv.at[far])
        part = y_out[far, y].astype(F32)
        for step in range(1, NY):
            part += y_got[far, step].astype(F32)
        if far:
            z_out[far] = part.astype(BF)
            z_copy(far).start()
        else:
            sum_ref[...] = part

    def pair_copy(section):
        view = whole_ref.at[section, :, core]
        return pltpu.make_async_remote_copy(
            src_ref=view,
            dst_ref=view,
            send_sem=pair_send.at[section],
            recv_sem=pair_recv.at[section],
            device_id={"dp_2": other},
            device_id_type=MESH,
        )

    for section in reversed(range(1, sections)):

        @pl.when(me < section)
        def _(section=section):
            took(whole_ref.at[section, pl.ds(0, 3), core], wide_recv.at[section])
            pair_copy(section).start()

    for far in range(1, ND):
        z_copy(far).wait_recv()
    result = sum_ref[...]
    for far in range(1, ND):
        result += z_got[far].astype(F32)
    sum_ref[...] = result

    @pl.when(is_relay)
    def _():
        took(moved_ref.at[:, pl.ds(0, RELAYS - 1)], moved_recv)
        sent(picked.at[pl.ds(0, replicas - 1)], moved_send)
        sent(spread.at[pl.ds(0, RELAYS - 1)], spread_send)

    @pl.when(jnp.logical_not(is_relay))
    def _():
        took(moved_ref, moved_recv)
        sent(spread.at[pl.ds(0, RELAYS)], spread_send)

    @pl.when(me < hop)
    def _():
        rows_copy().wait_send()

    @pl.when(valid)
    def _():
        sent(prod.at[0, pl.ds(0, replicas - 1)], prod_send)

    sent(uv_out.at[pl.ds(0, sections - 1)], uv_send)
    for section in range(sections):

        @pl.when(me != section)
        def _(section=section):
            p_copy(section).wait_send()

    for section in range(1, sections):

        @pl.when(me == section)
        def _(section=section):
            sent(prod.at[pl.ds(0, sections - 1), pl.ds(0, 4 * section)], gather_send)
            sent(whole_ref.at[pl.ds(0, section), 0, 0], slice_send)

        @pl.when(me < section)
        def _(section=section):
            sent(whole_ref.at[section, pl.ds(0, 3), core], wide_send.at[section])
            pair_copy(section).wait()

    for far in range(ND):
        half_copy(far).wait_send()
        sent(y_got.at[far, pl.ds(1, NY - 1)], y_send.at[far])
        if far:
            z_copy(far).wait_send()


def final_kernel(
    spots_ref,
    base_ref,
    p_ref,
    whole_ref,
    own_ref,
    summed_ref,
    moved_ref,
    emitted_ref,
    update_ref,
    first_ref,
    second_ref,
    left,
    weights,
    extra,
):
    step = pl.program_id(0)
    section = spots_ref[0]
    my_block = spots_ref[1]
    micro_count, tok_rows, chunk = base_ref.shape
    lanes = p_ref.shape[2]
    tokens = micro_count * tok_rows
    rank = own_ref.shape[0]
    rows = update_ref.shape[0]
    groups = lanes // 128

    @pl.when(step == 0)
    def _():
        lane_section = lax.broadcasted_iota(jnp.int32, (tok_rows, lanes), 1) // rank
        for micro in range(micro_count):
            value = p_ref[spots_ref[2 + micro]]
            left[micro * tok_rows : (micro + 1) * tok_rows, :] = jnp.where(
                lane_section >= section, value, jnp.zeros_like(value)
            )
        mixed = jnp.concatenate(
            [summed_ref[pl.ds(rows + group, 4, stride=groups), :] for group in range(groups)],
            axis=1,
        )
        mixed = jnp.concatenate([mixed, jnp.zeros((12, lanes), F32)], axis=0)
        left[tokens:, :] = mixed.astype(BF)

    for place in range(lanes // rank):
        part = pl.ds(place * rank, rank)

        @pl.when(place < section)
        def _(part=part):
            weights[part, :] = jnp.zeros((rank, chunk), BF)

        @pl.when(place == section)
        def _(part=part):
            weights[part, :] = own_ref[...]

        @pl.when(place > section)
        def _(part=part):
            weights[part, :] = whole_ref[part, :]

    result = jnp.dot(left[...], weights[...], preferred_element_type=F32)
    for micro in range(micro_count):
        moved = result[micro * tok_rows : (micro + 1) * tok_rows]
        emitted_ref[micro] = (base_ref[spots_ref[2 + micro]].astype(F32) + moved).astype(BF)
    added = result[tokens : tokens + 4]
    for group in range(chunk // 128):
        extra[pl.ds(step * (chunk // 128) + group, 4, stride=rows // 4), :] = added[
            :, group * 128 : (group + 1) * 128
        ]

    @pl.when(step == pl.num_programs(0) - 1)
    def _():
        outward = (my_block >= NC * NY * ND // 2).astype(F32)
        main = summed_ref[:rows, :]
        grads = jnp.where(outward > 0, main + extra[...], main) / loss_scale
        first_next = beta_one * moved_ref[0] + (1.0 - beta_one) * grads
        second_next = beta_two * moved_ref[1] + (1.0 - beta_two) * grads * grads
        first_ref[...] = first_next
        second_ref[...] = second_next
        update_ref[...] = (
            first_next
            / (1.0 - beta_one**adam_step)
            / (jnp.sqrt(second_next / (1.0 - beta_two**adam_step)) + adam_eps)
        )


def vmem():
    return pl.BlockSpec(memory_space=pltpu.VMEM)


def smem():
    return pl.BlockSpec(memory_space=pltpu.SMEM)


def hbm():
    return pl.BlockSpec(memory_space=pl.ANY)


def run_drain(table, inputs, base, turned, weight_out, first, second):
    tokens, width = inputs.shape
    rank = turned.shape[0]
    sections = SECTIONS
    replicas = ND * NY * NC
    tok_rows = tokens // sections
    lanes = sections * rank
    half_blocks = replicas // 2
    rows = width * rank // half_blocks // 128
    extra = rank * lanes // 128 // half_blocks
    relay_rows = first.shape[2]
    dma = pltpu.SemaphoreType.DMA
    full = (rows + extra, 128)
    return pl.pallas_call(
        drain_kernel,
        out_shape=(
            jax.ShapeDtypeStruct((sections, tok_rows, lanes), BF),
            jax.ShapeDtypeStruct((2, RELAYS, relay_rows, 128), F32),
            jax.ShapeDtypeStruct((sections, NY, NC, 8, width), BF),
            jax.ShapeDtypeStruct(full, F32),
        ),
        in_specs=[smem()] + [hbm()] * 4 + [vmem()] * 4,
        out_specs=(vmem(), vmem(), hbm(), vmem()),
        scratch_shapes=[
            pltpu.VMEM((tokens, width), BF),
            pltpu.VMEM((tokens, width), BF),
            pltpu.VMEM((tokens, rank), F32),
            pltpu.VMEM((tokens, rank), F32),
            pltpu.VMEM((tokens, rank), BF),
            pltpu.VMEM((2, 8, width), BF),
            pltpu.VMEM((8, 128), BF),
            pltpu.VMEM((sections, 32, 8, 128), BF),
            pltpu.VMEM((sections, tok_rows, 2 * rank), BF),
            pltpu.VMEM((sections, tok_rows, 2 * rank), BF),
            pltpu.VMEM((tok_rows, lanes), F32),
            pltpu.VMEM((replicas, 2, 2, relay_rows, 128), F32),
            pltpu.VMEM((replicas, 2, relay_rows, 128), F32),
            pltpu.VMEM((width, rank), F32),
            pltpu.VMEM((half_blocks * rows, 128), F32),
            pltpu.VMEM((half_blocks * extra, 128), F32),
            pltpu.VMEM((replicas, *full), F32),
            pltpu.VMEM((ND, NY, *full), BF),
            pltpu.VMEM((ND, NY, *full), BF),
            pltpu.VMEM((ND, NY, *full), BF),
            pltpu.VMEM((ND, NY, *full), BF),
            pltpu.VMEM((ND, *full), BF),
            pltpu.VMEM((ND, *full), BF),
            dma((2, 6)),
            dma,
            dma,
            dma,
            dma,
            dma,
            dma,
            dma,
            dma((sections,)),
            dma((sections,)),
            dma,
            dma,
            dma,
            dma,
            dma,
            dma,
            dma((sections,)),
            dma((sections,)),
            dma((sections,)),
            dma((sections,)),
            dma((sections,)),
            dma((ND,)),
            dma((ND,)),
            dma((ND,)),
            dma((ND,)),
            dma((ND,)),
            dma((ND,)),
        ],
        compiler_params=pltpu.CompilerParams(
            collective_id=0, has_side_effects=True, vmem_limit_bytes=60 * 2**20
        ),
        name="drain",
    )(
        table,
        inputs,
        base,
        turned.reshape(NY, NC, 8, width),
        weight_out.reshape(2, rank // 16, 8, width),
        turned,
        weight_out,
        first,
        second,
    )


def run_final(spots, base, p_all, whole, own, summed, moved):
    micro_count, tok_rows, width = base.shape
    lanes = p_all.shape[2]
    tokens = micro_count * tok_rows
    rank = own.shape[0]
    rows = moved.shape[1]
    steps = 7
    chunk = width // steps
    row_shape = jax.ShapeDtypeStruct((rows, 128), F32)
    row_spec = pl.BlockSpec((rows, 128), lambda i: (0, 0))
    return pl.pallas_call(
        final_kernel,
        grid=(steps,),
        out_shape=(
            jax.ShapeDtypeStruct((micro_count, tok_rows, width), BF),
            row_shape,
            row_shape,
            row_shape,
        ),
        in_specs=[
            smem(),
            pl.BlockSpec((micro_count, tok_rows, chunk), lambda i: (0, 0, i)),
            pl.BlockSpec(p_all.shape, lambda i: (0, 0, 0)),
            pl.BlockSpec((lanes, chunk), lambda i: (0, i)),
            pl.BlockSpec((rank, chunk), lambda i: (0, i)),
            pl.BlockSpec(summed.shape, lambda i: (0, 0)),
            pl.BlockSpec(moved.shape, lambda i: (0, 0, 0)),
        ],
        out_specs=(
            pl.BlockSpec((micro_count, tok_rows, chunk), lambda i: (0, 0, i)),
            row_spec,
            row_spec,
            row_spec,
        ),
        scratch_shapes=[
            pltpu.VMEM((tokens + 16, lanes), BF),
            pltpu.VMEM((lanes, chunk), BF),
            pltpu.VMEM((rows, 128), F32),
        ],
        name="final",
    )(spots, base, p_all, whole, own, summed, moved)


def per_device(
    activations,
    loss_grads,
    adapter_in,
    adapter_out,
    first_moment,
    second_moment,
    old_owner,
    new_owner,
    plan,
):
    sections = lax.axis_size("section")
    section_index = lax.axis_index("section")
    replicas = lax.axis_size(DP)
    my_index = lax.axis_index(DP)
    micro_count, tok_rows, width = activations.shape[1:]
    rank = adapter_in.shape[2]
    tokens = micro_count * tok_rows
    inputs = activations[0].reshape(tokens, width)
    base = loss_grads.reshape(tokens, width)
    owners_old = old_owner[0]
    owners_new = new_owner[0]
    block_len = first_moment.shape[2] // 2
    block_rows = block_len // 128
    relay_rows = block_rows // RELAYS
    replica_ids = jnp.arange(replicas, dtype=jnp.int32)

    dest = replica_ids.reshape(ND, NY, NC).transpose(2, 0, 1).reshape(-1)
    owner_match = owners_new[None, :] == jnp.concatenate([replica_ids, dest, my_index[None]])[:, None]
    inverse_all = jnp.sum(jnp.where(owner_match, replica_ids[None, :], 0), axis=1)
    inverse = inverse_all[:replicas]
    old_match = (inverse // 2)[:, None] == jnp.arange(owners_old.shape[0], dtype=jnp.int32)[None, :]
    from_row = jnp.sum(jnp.where(old_match, owners_old[None, :], 0), axis=1)
    table = jnp.stack([from_row, inverse % 2, inverse_all[replicas : 2 * replicas]])
    spots = jnp.concatenate([section_index[None], inverse_all[2 * replicas :], plan])

    turned = adapter_in[0].T
    p_all, moved, whole, summed = run_drain(
        table.astype(jnp.int32),
        inputs,
        base,
        turned,
        adapter_out[0],
        first_moment.reshape(2, RELAYS, relay_rows, 128),
        second_moment.reshape(2, RELAYS, relay_rows, 128),
    )
    emitted, update, first_next, second_next = run_final(
        spots.astype(jnp.int32),
        loss_grads,
        p_all,
        whole.reshape(sections * rank, width),
        turned,
        summed,
        moved.reshape(2, block_rows, 128),
    )
    shape = (1, 1, block_len)
    return (
        emitted[None],
        update.reshape(shape),
        first_next.reshape(shape),
        second_next.reshape(shape),
    )


def solution(mesh):
    torus = Mesh(
        mesh.devices.reshape(mesh.shape["section"], ND, NY, NC), ("section", "dp_0", "dp_1", "dp_2")
    )
    in_specs = (
        P("section", None, DP, None),
        P(None, DP, None),
        P("section", None, None),
        P("section", None, None),
        P("section", DP, None),
        P("section", DP, None),
        P("section", None),
        P("section", None),
        P(),
    )
    out_specs = (
        P("section", None, DP, None),
        P("section", DP, None),
        P("section", DP, None),
        P("section", DP, None),
    )
    return jax.shard_map(
        per_device, mesh=torus, in_specs=in_specs, out_specs=out_specs, check_vma=False
    )
```

time: 605 us -> 92.4 us (0.15)
  waiting for transfers between devices: 281 us -> 0 us
  Pallas kernels: 0 us -> 85.9 us
  matrix products: 84.5 us -> 0 us
  local copies, waits for them, and re-layouts: 74.6 us -> 0.67 us
  starting transfers between devices: 55 us -> 0 us
  other arithmetic: 56.8 us -> 4.14 us
  loops' own time: 31.7 us -> 0 us
  between operations: 17 us -> 0.66 us
    unnamed x4 -> x0, waiting for transfers between devices: 154 us -> none
    ppermute x15 -> x0, waiting for transfers between devices: 107 us -> none  [passed_along(): lax.ppermute(value, axis, [(source, source + steps) for source in range(f...]
    pallas_call x0 -> x2, Pallas kernels: none -> 85.9 us  [the longest x1 75.8 us: run_drain(): pl.pallas_call(drain_kernel, out_shape=(jax.ShapeDtypeStruct((sections, t...]
    dot_general x77 -> x0, matrix products: 84.5 us -> none  [the longest x15 26.1 us: drain_turn(): jnp.dot(section_input.T, pre_grad, preferred_element_type=jnp.float32)]
    another operation x1 -> x0, loops' own time: 31.7 us -> none  [per_device(): lax.fori_loop(0, micro_count + sections - 1, drain_turn, start_state)]
    ppermute x15 -> x0, starting transfers between devices: 29.5 us -> none  [passed_along(): lax.ppermute(value, axis, [(source, source + steps) for source in range(f...]
    while x15 -> x0, other arithmetic: 27.3 us -> none
    dynamic_slice x30 -> x0, local copies, waits for them, and re-layouts: 26.1 us -> none  [the longest x15 16.2 us: drain_turn(): earlier = lax.dynamic_index_in_dim(emitted, clamped, 0, keepdims=False)]
  transfers between devices with their start and end apart: 20 -> 0, of which waited for: 19 -> 0; matrix products, arithmetic and copies ran while one was open for 10% -> 0% of each run, Pallas kernels for 0% -> 0%
where the time goes in v1:
time: 92.4 us; the launch traced here: 91.3 us
  Pallas kernels  85.9 us (93%)
  other arithmetic  4.14 us (4%)
    pallas_call x1, Pallas kernels, run_drain(): pl.pallas_call(drain_kernel, out_shape=(jax.ShapeDtypeStruct((sections, t...  75.8 us
    pallas_call x1, Pallas kernels, run_final(): pl.pallas_call(final_kernel, grid=(steps,), out_shape=(jax.ShapeDtypeStru...  10.1 us
    concatenate x1, other arithmetic, per_device(): jnp.concatenate([section_index[None], inverse_all[2 * replicas:], plan])  1.9 us

profile of v1, /device:TPU:6, one launch (start us, length us, event | category | flops | bytes accessed | tf_op | source)
XLA Modules:
  0.0 91.3 jit_solution(15646752543694812108)
XLA Ops:
  0.7 0.1 reshape.70
  0.7 0.1 pad_add_fusion.1
  0.8 0.8 select_reduce_fusion
  1.6 0.6 slice.9
  2.2 1.9 %pad_add_fusion.2.spots_ref = s32[10]{0:T(128)} fusion(s32[8]{0:T(128)} %param.17, s32[1]{0:T(128)} %slice.9, s32[1]{0:T(128)} %bitcast), kind=kLoop, calls=%fused_computation.12 | loop fusion | flops 20 | bytes 80 | tf_op jit(solution)/shard_map/concatenate | solution.py:828
  4.1 0.1 and_select_fusion.1
  4.1 0.7 select_reduce_fusion.1
  4.9 0.6 pad_add_fusion.table_ref
  5.5 75.8 %drain.1 = (bf16[8,48,512]{2,1,0:T(8,128)(2,1)}, f32[2,7,24,128]{3,2,1,0:T(8,128)}, bf16[8,4,2,8,5376]{4,3,2,1,0:T(8,128)(2,1)}, f32[184,128]{1,0:T(8,128)}) custom-call(s32[3,32]{1,0:T(4,128)} %pad_add_fusion.table_ref, bf16[384,5376]{1,0:T(8,128)(2,1)} %bitcast.31, bf16[384,5376]{1,0:T(8,128)(2,1)} %bitcast.26, bf16[4,2,8,5376]{3,2,1,0:T(8,128)(2,1)} %bitcast.27, ...), custom_call_target="tpu_custom_call" | custom-call | tf_op jit(solution)/shard_map/drain/pallas_call | solution.py:672
  81.3 10.1 %final.1 = (bf16[8,48,5376]{2,1,0:T(8,128)(2,1)}, f32[168,128]{1,0:T(8,128)}, f32[168,128]{1,0:T(8,128)}, f32[168,128]{1,0:T(8,128)}) custom-call(s32[10]{0:T(128)} %pad_add_fusion.2.spots_ref, bf16[8,48,5376]{2,1,0:T(8,128)(2,1)} %base_ref.1, bf16[8,48,512]{2,1,0:T(8,128)(2,1)} %get-tuple-element.12.p_ref, bf16[512,5376]{1,0:T(8,128)(2,1)} %bitcast.30, ...), custom_call_target="tpu_custom_call" | custom-call | tf_op jit(solution)/shard_map/final/pallas_call | solution.py:761
  (3 shorter events, 0.0 us)

commit v2 on v1

v2 whole, which is shorter than its diff:
```python
import functools

import jax
import jax.numpy as jnp
from jax import lax
from jax.experimental import pallas as pl
from jax.experimental.pallas import tpu as pltpu
from jax.sharding import Mesh
from jax.sharding import PartitionSpec as P

DP = ("dp_0", "dp_1", "dp_2")
ND, NY, NC = 4, 4, 2
SECTIONS = 8
RELAYS = 7
ALONG_Z = (1, 3, 5)
MESH = pl.DeviceIdType.MESH
BF = jnp.bfloat16
F32 = jnp.float32

beta_one = 0.9
beta_two = 0.95
adam_eps = 1e-08
adam_step = 1000.0
loss_scale = 4096.0


def dp_coords(index):
    return {"dp_0": index // (NY * NC), "dp_1": lax.rem(index // NC, NY), "dp_2": lax.rem(index, NC)}


def relay_spot(index):
    return 4 * index + index % 4


def drain_kernel(
    table_ref,
    inputs_ref,
    base_ref,
    weight_in_ref,
    weight_out_ref,
    first_ref,
    second_ref,
    emitted_ref,
    update_ref,
    next_first_ref,
    next_second_ref,
    inputs,
    base,
    pre_sum,
    act_sum,
    hidden,
    rows_got,
    packed,
    prod,
    uv_out,
    uv_got,
    total,
    moments,
    spread,
    picked,
    moved,
    whole,
    p_got,
    left,
    out,
    grad,
    flat,
    mixed_rows,
    extra_rows,
    held,
    half_out,
    half_got,
    y_out,
    y_got,
    z_out,
    z_got,
    summed,
    load_sem,
    rows_send,
    rows_recv,
    prod_send,
    prod_recv,
    uv_send,
    uv_recv,
    gather_send,
    gather_recv,
    p_send,
    p_recv,
    spread_send,
    spread_recv,
    moved_send,
    moved_recv,
    slice_send,
    slice_recv,
    wide_send,
    wide_recv,
    pair_send,
    pair_recv,
    half_send,
    half_recv,
    y_send,
    y_recv,
    z_send,
    z_recv,
    out_sem,
):
    sections = SECTIONS
    replicas = ND * NY * NC
    me = lax.axis_index("section")
    z = lax.axis_index("dp_0")
    y = lax.axis_index("dp_1")
    core = lax.axis_index("dp_2")
    dp = (z * NY + y) * NC + core
    other = 1 - core
    tokens, width = inputs.shape
    rank = weight_in_ref.shape[0]
    tok_rows = tokens // sections
    lanes = sections * rank
    parts = load_sem.shape[1]
    chunk = width // parts
    groups = chunk // 128
    block_rows = flat.shape[0] // (replicas // 2)
    half_blocks = replicas // 2
    extra = held.shape[1] - block_rows
    relay_rows = first_ref.shape[2]
    tall = rank // NY
    wide = width // NC

    def load(which, part):
        columns = pl.ds(pl.multiple_of(part * chunk, 128), chunk)
        if which == 0:
            source, target = inputs_ref.at[:, columns], inputs.at[:, columns]
        else:
            source, target = base_ref.at[:, :, columns], base.at[:, :, columns]
        return pltpu.make_async_copy(source, target, load_sem.at[which, part])

    for part in range(parts):
        load(0, part).start()
        load(1, part).start()

    barrier = pltpu.get_barrier_semaphore()
    for step in range(1, sections):
        pl.semaphore_signal(
            barrier, inc=1, device_id={"section": lax.rem(me + step, sections)}, device_id_type=MESH
        )

    def greet(step, carry):
        pl.semaphore_signal(
            barrier, inc=1, device_id=dp_coords(lax.rem(dp + step, replicas)), device_id_type=MESH
        )
        return carry

    lax.fori_loop(1, replicas, greet, 0)

    for index in range(RELAYS):
        for which, source in enumerate((first_ref, second_ref)):
            for half in range(2):
                start = (2 * which + half) * relay_rows
                moments[index, start : start + relay_rows, :] = source[half, index].astype(BF)

    for section in range(sections):

        @pl.when(section < me)
        def _(section=section):
            whole[pl.ds(section * rank, rank), :] = jnp.zeros((rank, width), BF)

        @pl.when(section == me)
        def _(section=section):
            whole[pl.ds(section * rank, rank), :] = weight_in_ref[...]

    pl.semaphore_wait(barrier, sections - 1 + replicas - 1)

    def section_copy(src, dst, send, recv, target):
        return pltpu.make_async_remote_copy(
            src_ref=src,
            dst_ref=dst,
            send_sem=send,
            recv_sem=recv,
            device_id={"section": target},
            device_id_type=MESH,
        )

    def took(view, sem):
        section_copy(view, view, sem, sem, me).wait_recv()

    def sent(view, sem):
        section_copy(view, view, sem, sem, me).wait_send()

    hop = dp // 4

    def rows_copy():
        return section_copy(
            weight_out_ref.at[pl.ds(pl.multiple_of(lax.rem(dp, 4) * tall, tall), tall)],
            rows_got,
            rows_send,
            rows_recv,
            lax.rem(me + sections - hop, sections),
        )

    @pl.when(me < hop)
    def _():
        rows_copy().start()

    def along_z(section):
        return lax.rem(section, 2) * (1 - section // 7)

    def row_of(section):
        return y + along_z(section) * (z - y)

    def slice_view(ref, section, row):
        start = pl.multiple_of(section * rank + row * tall, tall)
        return ref.at[pl.ds(start, tall), pl.ds(pl.multiple_of(core * wide, 128), wide)]

    relay = dp // 4
    is_relay = (lax.rem(dp, 4) == lax.rem(relay, 4)) & (relay < RELAYS)

    def spread_copy(index):
        peer = relay_spot(index)
        return pltpu.make_async_remote_copy(
            src_ref=moments.at[index],
            dst_ref=spread.at[dp],
            send_sem=spread_send,
            recv_sem=spread_recv,
            device_id={"dp_0": peer // 8, "dp_1": peer // 2 % 4, "dp_2": peer % 2},
            device_id_type=MESH,
        )

    across = (((1,), (1,)), ((), ()))
    down = (((0,), (0,)), ((), ()))
    pre_sum[...] = jnp.zeros_like(pre_sum)
    act_sum[...] = jnp.zeros_like(act_sum)

    def accumulate(part, carry):
        columns = pl.ds(pl.multiple_of(part * chunk, 128), chunk)
        load(0, part).wait()
        pre_sum[...] += lax.dot_general(
            inputs[:, columns], weight_in_ref[:, columns], across, preferred_element_type=F32
        )
        load(1, part).wait()
        act_sum[...] += lax.dot_general(
            base[:, :, columns].reshape(tokens, chunk),
            weight_out_ref[:, columns],
            across, preferred_element_type=F32
        )
        return carry

    lax.fori_loop(0, parts, accumulate, 0)
    pre_value = pre_sum[...]
    gate = jax.nn.sigmoid(pre_value)
    hidden[...] = (pre_value * gate).astype(BF)
    slope = gate * (1.0 + pre_value * (1.0 - gate))
    both = jnp.concatenate([act_sum[...].astype(BF), slope.astype(BF)], axis=1)
    uv_out[...] = both.reshape(sections, tok_rows, 2 * rank)

    def uv_copy(step):
        target = lax.rem(me + step, sections)
        return section_copy(uv_out.at[target], uv_got.at[me], uv_send, uv_recv, target)

    for step in range(1, sections):
        uv_copy(step).start()
    uv_got[me] = uv_out[me]

    slot = lax.rem(hop + me, sections) * 4 + lax.rem(dp, 4)
    valid = me + hop >= sections

    def prod_copy(step):
        return pltpu.make_async_remote_copy(
            src_ref=packed,
            dst_ref=prod.at[me, slot],
            send_sem=prod_send,
            recv_sem=prod_recv,
            device_id=dp_coords(lax.rem(dp + step, replicas)),
            device_id_type=MESH,
        )

    @pl.when(valid)
    def _():
        took(rows_got, rows_recv)
        piece = lax.dot_general(
            rows_got[...], weight_in_ref[...], across, preferred_element_type=F32
        )
        packed[...] = jnp.concatenate([piece[:8], piece[8:]], axis=1).astype(BF)

        def prod_start(step, carry):
            prod_copy(step).start()
            return carry

        lax.fori_loop(1, replicas, prod_start, 0)
        prod[me, slot] = packed[...]

    for section in range(1, sections):

        @pl.when(me == section)
        def _(section=section):
            row = z if section in ALONG_Z else y
            for target in reversed(range(section)):
                section_copy(
                    slice_view(weight_in_ref, 0, row),
                    slice_view(whole, section, row),
                    slice_send,
                    slice_recv.at[section],
                    target,
                ).start()

    for index in range(RELAYS):

        @pl.when(dp != relay_spot(index))
        def _(index=index):
            spread_copy(index).start()

        @pl.when(dp == relay_spot(index))
        def _(index=index):
            spread[relay_spot(index)] = moments[index]

    def outward(part, carry):
        columns = pl.ds(pl.multiple_of(part * chunk, 128), chunk)
        result = lax.dot_general(
            hidden[...],
            base[:, :, columns].reshape(tokens, chunk),
            down,
            preferred_element_type=F32,
        )
        for group in range(groups):
            flat[pl.ds(part * groups + group, rank, stride=width // 128), :] = result[
                :, group * 128 : (group + 1) * 128
            ]
        return carry

    lax.fori_loop(0, parts, outward, 0)
    for block in range(half_blocks):
        held[half_blocks + block, :block_rows] = flat[pl.ds(block * block_rows, block_rows), :]

    for section in range(1, sections):

        @pl.when((me == section) & valid)
        def _(section=section):
            took(prod.at[0, pl.ds(0, 4 * section - 1)], prod_recv)

        @pl.when((me == section) & (me + hop < sections))
        def _(section=section):
            took(prod.at[0, pl.ds(0, 4 * section)], prod_recv)

        @pl.when(me == section)
        def _(section=section):
            for step in range(1, sections):
                section_copy(
                    prod.at[section, pl.ds(0, 4 * section)],
                    prod.at[section, pl.ds(0, 4 * section)],
                    gather_send,
                    gather_recv.at[section],
                    (section - step) % sections,
                ).start()

    def wide_copy(section, shift):
        view = slice_view(whole, section, row_of(section))
        axis, at, count = ("dp_0", z, ND) if section in ALONG_Z else ("dp_1", y, NY)
        return pltpu.make_async_remote_copy(
            src_ref=view,
            dst_ref=view,
            send_sem=wide_send.at[section],
            recv_sem=wide_recv.at[section],
            device_id={axis: lax.rem(at + shift, count)},
            device_id_type=MESH,
        )

    def spread_adapters(chosen):
        for section in chosen:

            @pl.when(me < section)
            def _(section=section):
                took(slice_view(whole, section, row_of(section)), slice_recv.at[section])
                for shift in (1, 3, 2):
                    wide_copy(section, shift).start()

    spread_adapters([section for section in range(1, sections) if section not in ALONG_Z])

    def moved_copy(step):
        peer = lax.rem(dp + step, replicas)
        return pltpu.make_async_remote_copy(
            src_ref=picked.at[peer],
            dst_ref=moved.at[relay],
            send_sem=moved_send,
            recv_sem=moved_recv,
            device_id=dp_coords(peer),
            device_id_type=MESH,
        )

    took(uv_got.at[pl.ds(0, sections - 1)], uv_recv)
    for section in range(1, sections):

        @pl.when(me != section)
        def _(section=section):
            took(prod.at[section, pl.ds(0, 4 * section)], gather_recv.at[section])

    total[...] = jnp.zeros_like(total)
    for turn in reversed(range(sections)):
        low, high = turn * rank, (turn + 1) * rank
        pair = uv_got[turn].astype(F32)
        p_value = ((pair[:, :rank] + total[:, low:high]) * pair[:, rank:]).astype(BF)
        p_got[me, :, low:high] = p_value
        if turn:
            got = prod[turn, : 4 * turn].astype(F32)
            rows = jnp.concatenate([got[:, :, :rank], got[:, :, rank:]], axis=1)
            rows = rows.reshape(turn * rank, rank).astype(BF)
            total[:, :low] += lax.dot_general(p_value, rows, across, preferred_element_type=F32)

    def live(section):
        start = section // 2 * 2 * rank
        return pl.ds(start, lanes - start)

    def p_copy(section):
        view = p_got.at[me, :, live(section)]
        return section_copy(view, view, p_send.at[section], p_recv, section)

    for section in range(sections):

        @pl.when(me != section)
        def _(section=section):
            p_copy(section).start()

    spread_adapters(ALONG_Z)

    @pl.when(is_relay)
    def _():
        took(spread.at[pl.ds(0, replicas - 1)], spread_recv)

        def pick(target, carry):
            rows = spread[table_ref[0, target]].astype(F32)
            upper = table_ref[1, target] > 0
            for which in range(2):
                start = 2 * which * relay_rows
                low = rows[start : start + relay_rows]
                high = rows[start + relay_rows : start + 2 * relay_rows]
                picked[target, which * relay_rows : (which + 1) * relay_rows, :] = jnp.where(
                    upper, high, low
                ).astype(BF)
            return carry

        lax.fori_loop(0, replicas, pick, 0)

        def moved_start(step, carry):
            moved_copy(step).start()
            return carry

        lax.fori_loop(1, replicas, moved_start, 0)
        moved[relay] = picked[dp]

    for section in range(sections):

        @pl.when(me == section)
        def _(section=section):
            took(p_got.at[pl.ds(0, sections - 1), :, live(section)], p_recv)

    lane_section = lax.broadcasted_iota(jnp.int32, (tokens, lanes), 1) // rank
    p_all = p_got[...].reshape(tokens, lanes)
    p_above = jnp.where(lane_section > me, p_all, jnp.zeros_like(p_all))
    p_live = jnp.where(lane_section == me, p_all, jnp.zeros_like(p_all))
    take = lax.rem(lax.broadcasted_iota(jnp.int32, (lanes, rank), 0), rank) == (
        lax.broadcasted_iota(jnp.int32, (lanes, rank), 1)
    )
    p_mine = jnp.dot(p_live, take.astype(F32).astype(BF), preferred_element_type=F32).astype(BF)

    def inward(part, carry):
        columns = pl.ds(pl.multiple_of(part * chunk, 128), chunk)
        grad[columns, :] = lax.dot_general(
            inputs[:, columns], p_mine, down, preferred_element_type=F32
        )
        return carry

    lax.fori_loop(0, parts, inward, 0)
    mixed = lax.dot_general(hidden[...], p_above, down, preferred_element_type=F32)
    for group in range(lanes // 128):
        mixed_rows[pl.ds(group, rank, stride=lanes // 128), :] = mixed[
            :, group * 128 : (group + 1) * 128
        ]
    for block in range(half_blocks):
        even = grad[pl.ds(block * 2 * block_rows, block_rows, stride=2), :]
        odd = grad[pl.ds(block * 2 * block_rows + 1, block_rows, stride=2), :]
        held[block, :block_rows] = jnp.concatenate([even, odd], axis=1)
        held[block, block_rows:] = jnp.zeros((extra, 128), F32)
        held[half_blocks + block, block_rows:] = mixed_rows[pl.ds(block * extra, extra), :]

    order = (2, 1, 3, 0)

    def half_copy(far):
        return pltpu.make_async_remote_copy(
            src_ref=half_out.at[far],
            dst_ref=half_got.at[far],
            send_sem=half_send.at[far],
            recv_sem=half_recv.at[far],
            device_id={"dp_2": other},
            device_id_type=MESH,
        )

    def y_copy(far, step):
        there = lax.rem(y + step, NY)
        return pltpu.make_async_remote_copy(
            src_ref=y_out.at[far, there],
            dst_ref=y_got.at[far, step],
            send_sem=y_send.at[far],
            recv_sem=y_recv.at[far],
            device_id={"dp_1": there},
            device_id_type=MESH,
        )

    def z_copy(far):
        return pltpu.make_async_remote_copy(
            src_ref=z_out.at[far],
            dst_ref=z_got.at[far],
            send_sem=z_send.at[far],
            recv_sem=z_recv.at[far],
            device_id={"dp_0": lax.rem(z + far, ND)},
            device_id_type=MESH,
        )

    for far in order:
        there = lax.rem(z + far, ND)
        for column in range(NY):
            half_out[far, column] = held[table_ref[2, (other * ND + there) * NY + column]].astype(BF)
        half_copy(far).start()
    for far in order:
        there = lax.rem(z + far, ND)
        half_copy(far).wait_recv()
        for column in range(NY):
            own = held[table_ref[2, (core * ND + there) * NY + column]]
            y_out[far, column] = (own + half_got[far, column].astype(F32)).astype(BF)
        for step in (2, 1, 3):
            y_copy(far, step).start()
    def pair_copy(section):
        view = whole.at[
            pl.ds(section * rank, rank), pl.ds(pl.multiple_of(core * wide, 128), wide)
        ]
        return pltpu.make_async_remote_copy(
            src_ref=view,
            dst_ref=view,
            send_sem=pair_send.at[section],
            recv_sem=pair_recv.at[section],
            device_id={"dp_2": other},
            device_id_type=MESH,
        )

    place = lax.broadcasted_iota(jnp.int32, (tok_rows, lanes), 1) // rank
    for micro in range(sections):
        value = p_got[table_ref[3, micro]]
        left[micro * tok_rows : (micro + 1) * tok_rows, :] = jnp.where(
            place >= me, value, jnp.zeros_like(value)
        )

    for section in range(1, sections):

        @pl.when(me < section)
        def _(section=section):
            took(
                whole.at[pl.ds(section * rank, 3 * tall), pl.ds(0, wide)], wide_recv.at[section]
            )
            pair_copy(section).start()

    for far in order:
        took(y_got.at[far, pl.ds(1, NY - 1)], y_recv.at[far])
        part = y_out[far, y].astype(F32)
        for step in range(1, NY):
            part += y_got[far, step].astype(F32)
        if far:
            z_out[far] = part.astype(BF)
            z_copy(far).start()
        else:
            summed[...] = part

    for section in range(1, sections):

        @pl.when(me < section)
        def _(section=section):
            pair_copy(section).wait_recv()

    slabs = out_sem.shape[0]
    slab = width // slabs

    def out_copy(index):
        columns = pl.ds(pl.multiple_of(index * slab, 128), slab)
        return pltpu.make_async_copy(
            out.at[:, :, columns], emitted_ref.at[:, :, columns], out_sem.at[index]
        )

    def emit(index, carry):
        columns = pl.ds(pl.multiple_of(index * slab, 128), slab)
        result = jnp.dot(left[...], whole[:, columns], preferred_element_type=F32)
        for micro in range(sections):
            added = result[micro * tok_rows : (micro + 1) * tok_rows]
            out[micro, :, columns] = (
                base[table_ref[3, micro], :, columns].astype(F32) + added
            ).astype(BF)
        out_copy(index).start()
        return carry

    lax.fori_loop(0, slabs, emit, 0)

    for far in range(1, ND):
        z_copy(far).wait_recv()
    result = summed[...]
    for far in range(1, ND):
        result += z_got[far].astype(F32)
    summed[...] = result

    apart = lanes // 128
    mixed = jnp.concatenate(
        [summed[pl.ds(block_rows + group, 4, stride=apart), :] for group in range(apart)], axis=1
    )
    mixed = jnp.concatenate([mixed, jnp.zeros((12, lanes), F32)], axis=0).astype(BF)

    def correct(index, carry):
        columns = pl.ds(pl.multiple_of(index * slab, 128), slab)
        result = jnp.dot(mixed, whole[:, columns], preferred_element_type=F32)
        for group in range(slab // 128):
            extra_rows[pl.ds(index * (slab // 128) + group, 4, stride=width // 128), :] = result[
                :4, group * 128 : (group + 1) * 128
            ]
        return carry

    lax.fori_loop(0, slabs, correct, 0)

    @pl.when(is_relay)
    def _():
        took(moved.at[pl.ds(0, RELAYS - 1)], moved_recv)
        sent(picked.at[pl.ds(0, replicas - 1)], moved_send)
        sent(spread.at[pl.ds(0, RELAYS - 1)], spread_send)

    @pl.when(jnp.logical_not(is_relay))
    def _():
        took(moved, moved_recv)
        sent(spread.at[pl.ds(0, RELAYS)], spread_send)

    is_out = table_ref[4, 0] >= half_blocks
    main = summed[:block_rows, :]
    grads = jnp.where(is_out, main + extra_rows[...], main) / loss_scale
    for index in range(RELAYS):
        at = slice(index * relay_rows, (index + 1) * relay_rows)
        old = moved[index].astype(F32)
        g = grads[at]
        first_next = beta_one * old[:relay_rows] + (1.0 - beta_one) * g
        second_next = beta_two * old[relay_rows:] + (1.0 - beta_two) * g * g
        next_first_ref[at, :] = first_next
        next_second_ref[at, :] = second_next
        update_ref[at, :] = (
            first_next
            / (1.0 - beta_one**adam_step)
            / (jnp.sqrt(second_next / (1.0 - beta_two**adam_step)) + adam_eps)
        )

    @pl.when(me < hop)
    def _():
        rows_copy().wait_send()

    @pl.when(valid)
    def _():
        sent(prod.at[0, pl.ds(0, replicas - 1)], prod_send)

    sent(uv_out.at[pl.ds(0, sections - 1)], uv_send)
    for section in range(sections):

        @pl.when(me != section)
        def _(section=section):
            p_copy(section).wait_send()

    for section in range(1, sections):

        @pl.when(me == section)
        def _(section=section):
            sent(prod.at[pl.ds(0, sections - 1), pl.ds(0, 4 * section)], gather_send)
            sent(whole.at[pl.ds(0, section * tall), pl.ds(0, wide)], slice_send)

        @pl.when(me < section)
        def _(section=section):
            sent(whole.at[pl.ds(0, 3 * tall), pl.ds(0, wide)], wide_send.at[section])
            pair_copy(section).wait_send()

    for far in range(ND):
        half_copy(far).wait_send()
        sent(y_got.at[far, pl.ds(1, NY - 1)], y_send.at[far])
        if far:
            z_copy(far).wait_send()

    for index in range(slabs):
        out_copy(index).wait()


def vmem():
    return pl.BlockSpec(memory_space=pltpu.VMEM)


def smem():
    return pl.BlockSpec(memory_space=pltpu.SMEM)


def hbm():
    return pl.BlockSpec(memory_space=pl.ANY)


def run_drain(table, inputs, base, turned, weight_out, first, second):
    tokens, width = inputs.shape
    rank = turned.shape[0]
    sections = SECTIONS
    replicas = ND * NY * NC
    tok_rows = tokens // sections
    lanes = sections * rank
    half_blocks = replicas // 2
    rows = width * rank // half_blocks // 128
    extra = rank * lanes // 128 // half_blocks
    relay_rows = first.shape[2]
    dma = pltpu.SemaphoreType.DMA
    full = (rows + extra, 128)
    per_section = dma((sections,))
    per_z = dma((ND,))
    row_shape = jax.ShapeDtypeStruct((rows, 128), F32)
    return pl.pallas_call(
        drain_kernel,
        out_shape=(
            jax.ShapeDtypeStruct((sections, tok_rows, width), BF),
            row_shape,
            row_shape,
            row_shape,
        ),
        in_specs=[smem()] + [hbm()] * 2 + [vmem()] * 4,
        out_specs=(hbm(), vmem(), vmem(), vmem()),
        scratch_shapes=[
            pltpu.VMEM((tokens, width), BF),
            pltpu.VMEM((sections, tok_rows, width), BF),
            pltpu.VMEM((tokens, rank), F32),
            pltpu.VMEM((tokens, rank), F32),
            pltpu.VMEM((tokens, rank), BF),
            pltpu.VMEM((rank // NY, width), BF),
            pltpu.VMEM((8, 128), BF),
            pltpu.VMEM((sections, 32, 8, 128), BF),
            pltpu.VMEM((sections, tok_rows, 2 * rank), BF),
            pltpu.VMEM((sections, tok_rows, 2 * rank), BF),
            pltpu.VMEM((tok_rows, lanes), F32),
            pltpu.VMEM((RELAYS, 4 * relay_rows, 128), BF),
            pltpu.VMEM((replicas, 4 * relay_rows, 128), BF),
            pltpu.VMEM((replicas, 2 * relay_rows, 128), BF),
            pltpu.VMEM((RELAYS, 2 * relay_rows, 128), BF),
            pltpu.VMEM((lanes, width), BF),
            pltpu.VMEM((sections, tok_rows, lanes), BF),
            pltpu.VMEM((tokens, lanes), BF),
            pltpu.VMEM((sections, tok_rows, width), BF),
            pltpu.VMEM((width, rank), F32),
            pltpu.VMEM((half_blocks * rows, 128), F32),
            pltpu.VMEM((half_blocks * extra, 128), F32),
            pltpu.VMEM((rows, 128), F32),
            pltpu.VMEM((replicas, *full), F32),
            pltpu.VMEM((ND, NY, *full), BF),
            pltpu.VMEM((ND, NY, *full), BF),
            pltpu.VMEM((ND, NY, *full), BF),
            pltpu.VMEM((ND, NY, *full), BF),
            pltpu.VMEM((ND, *full), BF),
            pltpu.VMEM((ND, *full), BF),
            pltpu.VMEM(full, F32),
            dma((2, 6)),
            dma,
            dma,
            dma,
            dma,
            dma,
            dma,
            dma,
            per_section,
            per_section,
            dma,
            dma,
            dma,
            dma,
            dma,
            dma,
            per_section,
            per_section,
            per_section,
            per_section,
            per_section,
            per_z,
            per_z,
            per_z,
            per_z,
            per_z,
            per_z,
            dma((7,)),
        ],
        compiler_params=pltpu.CompilerParams(
            collective_id=0, has_side_effects=True, vmem_limit_bytes=60 * 2**20
        ),
        name="drain",
    )(table, inputs, base, turned, weight_out, first, second)


def per_device(
    activations,
    loss_grads,
    adapter_in,
    adapter_out,
    first_moment,
    second_moment,
    old_owner,
    new_owner,
    plan,
):
    replicas = lax.axis_size(DP)
    my_index = lax.axis_index(DP)
    micro_count, tok_rows, width = activations.shape[1:]
    rank = adapter_in.shape[2]
    tokens = micro_count * tok_rows
    inputs = activations[0].reshape(tokens, width)
    owners_old = old_owner[0]
    owners_new = new_owner[0]
    block_len = first_moment.shape[2] // 2
    block_rows = block_len // 128
    relay_rows = block_rows // RELAYS
    replica_ids = jnp.arange(replicas, dtype=jnp.int32)

    dest = replica_ids.reshape(ND, NY, NC).transpose(2, 0, 1).reshape(-1)
    owner_match = owners_new[None, :] == jnp.concatenate([replica_ids, dest, my_index[None]])[:, None]
    inverse_all = jnp.sum(jnp.where(owner_match, replica_ids[None, :], 0), axis=1)
    inverse = inverse_all[:replicas]
    old_match = (inverse // 2)[:, None] == jnp.arange(owners_old.shape[0], dtype=jnp.int32)[None, :]
    from_row = jnp.sum(jnp.where(old_match, owners_old[None, :], 0), axis=1)
    padded = jnp.concatenate([plan, jnp.zeros((replicas - micro_count,), jnp.int32)])
    my_block = jnp.broadcast_to(inverse_all[2 * replicas :], (replicas,))
    table = jnp.stack(
        [from_row, inverse % 2, inverse_all[replicas : 2 * replicas], padded, my_block]
    )
    emitted, update, first_next, second_next = run_drain(
        table.astype(jnp.int32),
        inputs,
        loss_grads,
        adapter_in[0].T,
        adapter_out[0],
        first_moment.reshape(2, RELAYS, relay_rows, 128),
        second_moment.reshape(2, RELAYS, relay_rows, 128),
    )
    shape = (1, 1, block_len)
    return (
        emitted[None],
        update.reshape(shape),
        first_next.reshape(shape),
        second_next.reshape(shape),
    )


def solution(mesh):
    torus = Mesh(
        mesh.devices.reshape(mesh.shape["section"], ND, NY, NC), ("section", "dp_0", "dp_1", "dp_2")
    )
    in_specs = (
        P("section", None, DP, None),
        P(None, DP, None),
        P("section", None, None),
        P("section", None, None),
        P("section", DP, None),
        P("section", DP, None),
        P("section", None),
        P("section", None),
        P(),
    )
    out_specs = (
        P("section", None, DP, None),
        P("section", DP, None),
        P("section", DP, None),
        P("section", DP, None),
    )
    return jax.shard_map(
        per_device, mesh=torus, in_specs=in_specs, out_specs=out_specs, check_vma=False
    )
```

time: 92.4 us -> 86.3 us (0.934)
  the two profiles are of different devices: /device:TPU:6 before, /device:TPU:17 now
where the time goes in v2:
time: 86.3 us; the launch traced here: 86.1 us
  Pallas kernels  74.8 us (87%)
  local copies, waits for them, and re-layouts  8.97 us (10%)
  other arithmetic  1.66 us (2%)
    pallas_call x1, Pallas kernels, run_drain(): pl.pallas_call(drain_kernel, out_shape=(jax.ShapeDtypeStruct((sections, t...  74.8 us
    unnamed x10, local copies, waits for them, and re-layouts  6.39 us
    another operation x3, local copies, waits for them, and re-layouts, per_device(): jnp.stack([from_row, inverse % 2, inverse_all[replicas:2 * replicas], pad...  1.92 us

profile of v2, /device:TPU:17, one launch (start us, length us, event | category | flops | bytes accessed | tf_op | source)
XLA Modules:
  0.0 86.1 jit_solution(3006882607749475302)
XLA Ops:
  0.6 0.7 pad_bitcast_fusion
  1.3 0.1 reshape.61
  1.4 0.1 pad_add_fusion
  1.5 0.7 select_reduce_fusion
  2.2 0.6 slice.13
  2.8 0.6 stack_broadcast_in_dim.2
  3.5 0.1 fusion
  3.5 0.7 select_reduce_fusion.1
  4.3 0.6 stack.19.table_ref
  4.9 74.8 %drain.1 = (bf16[8,48,5376]{2,1,0:T(8,128)(2,1)}, f32[168,128]{1,0:T(8,128)}, f32[168,128]{1,0:T(8,128)}, f32[168,128]{1,0:T(8,128)}) custom-call(s32[5,32]{1,0:T(8,128)} %stack.19.table_ref, bf16[384,5376]{1,0:T(8,128)(2,1)} %bitcast.22, bf16[8,48,5376]{2,1,0:T(8,128)(2,1)} %base_ref.1, bf16[64,5376]{1,0:T(8,128)(2,1)} %bitcast.24, ...), custom_call_target="tpu_custom_call" | custom-call | tf_op jit(solution)/shard_map/drain/pallas_call | solution.py:714
  79.7 0.0 copy-start.2
  79.7 0.0 copy-start.1
  79.8 0.0 copy-start
  79.8 4.5 %copy.17 = bf16[1,8,48,5376]{3,2,1,0:T(8,128)(2,1)} copy(bf16[1,8,48,5376]{3,2,1,0:T(8,128)(2,1)} %bitcast.23) | data formatting | bytes 8257536
  84.2 0.0 copy-done.2
  84.2 0.6 copy.18
  84.9 0.0 copy-done.1
  84.9 0.6 copy.19
  85.5 0.0 copy-done
  85.5 0.6 copy.20
  (3 shorter events, 0.0 us)
Async XLA Ops:
  79.7 4.5 %copy-start.2 = (f32[168,128]{1,0:T(8,128)S(1)}, f32[168,128]{1,0:T(8,128)}, u32[]{:S(2)}) copy-start(f32[168,128]{1,0:T(8,128)} %get-tuple-element.9) | copy-start | bytes 258052
  79.7 5.1 %copy-start.1 = (f32[168,128]{1,0:T(8,128)S(1)}, f32[168,128]{1,0:T(8,128)}, u32[]{:S(2)}) copy-start(f32[168,128]{1,0:T(8,128)} %get-tuple-element.10) | copy-start | bytes 258052
  79.8 5.8 %copy-start = (f32[168,128]{1,0:T(8,128)S(1)}, f32[168,128]{1,0:T(8,128)}, u32[]{:S(2)}) copy-start(f32[168,128]{1,0:T(8,128)} %get-tuple-element.11) | copy-start | bytes 258052

commit v3 on v2

--- a/solution.py
+++ b/solution.py
@@ -12,7 +12,7 @@
 ND, NY, NC = 4, 4, 2
 SECTIONS = 8
 RELAYS = 7
-ALONG_Z = (1, 3, 5)
+ALONG_Z = (1, 2,)
 MESH = pl.DeviceIdType.MESH
 BF = jnp.bfloat16
 F32 = jnp.float32
@@ -34,16 +34,17 @@
 
 def drain_kernel(
     table_ref,
+    old_ref,
+    plan_ref,
     inputs_ref,
     base_ref,
     weight_in_ref,
     weight_out_ref,
     first_ref,
     second_ref,
-    emitted_ref,
-    update_ref,
-    next_first_ref,
-    next_second_ref,
+    out,
+    grads_ref,
+    moved,
     inputs,
     base,
     pre_sum,
@@ -58,11 +59,9 @@
     moments,
     spread,
     picked,
-    moved,
     whole,
     p_got,
     left,
-    out,
     grad,
     flat,
     mixed_rows,
@@ -92,6 +91,7 @@
     moved_recv,
     slice_send,
     slice_recv,
+    pass_send,
     wide_send,
     wide_recv,
     pair_send,
@@ -102,7 +102,6 @@
     y_recv,
     z_send,
     z_recv,
-    out_sem,
 ):
     sections = SECTIONS
     replicas = ND * NY * NC
@@ -197,19 +196,40 @@
             lax.rem(me + sections - hop, sections),
         )
 
+    def slice_view(ref, section, row):
+        start = pl.multiple_of(section * rank + row * tall, tall)
+        return ref.at[pl.ds(start, tall), pl.ds(pl.multiple_of(core * wide, 128), wide)]
+
     @pl.when(me < hop)
     def _():
         rows_copy().start()
 
-    def along_z(section):
-        return lax.rem(section, 2) * (1 - section // 7)
+    half = sections // 2
+
+    def slice_copy(source, section, send, target):
+        row = z if section in ALONG_Z else y
+        start = 0 if source is weight_in_ref else section
+        return section_copy(
+            slice_view(source, start, row),
+            slice_view(whole, section, row),
+            send,
+            slice_recv.at[section],
+            target,
+        )
+
+    def slice_targets(section):
+        first = section // half * half
+        return [section - half] * (section >= half) + list(range(first, section))
+
+    for section in range(1, sections):
+
+        @pl.when(me == section)
+        def _(section=section):
+            for target in slice_targets(section):
+                slice_copy(weight_in_ref, section, slice_send, target).start()
 
     def row_of(section):
-        return y + along_z(section) * (z - y)
-
-    def slice_view(ref, section, row):
-        start = pl.multiple_of(section * rank + row * tall, tall)
-        return ref.at[pl.ds(start, tall), pl.ds(pl.multiple_of(core * wide, 128), wide)]
+        return z if section in ALONG_Z else y
 
     relay = dp // 4
     is_relay = (lax.rem(dp, 4) == lax.rem(relay, 4)) & (relay < RELAYS)
@@ -245,6 +265,15 @@
         return carry
 
     lax.fori_loop(0, parts, accumulate, 0)
+    for section in range(half):
+
+        @pl.when(me == section)
+        def _(section=section):
+            above = section + half
+            took(slice_view(whole, above, row_of(above)), slice_recv.at[above])
+            for step in (1, 3, 2):
+                slice_copy(whole, above, pass_send, (section + step) % half).start()
+
     pre_value = pre_sum[...]
     gate = jax.nn.sigmoid(pre_value)
     hidden[...] = (pre_value * gate).astype(BF)
@@ -287,30 +316,6 @@
 
         lax.fori_loop(1, replicas, prod_start, 0)
         prod[me, slot] = packed[...]
-
-    for section in range(1, sections):
-
-        @pl.when(me == section)
-        def _(section=section):
-            row = z if section in ALONG_Z else y
-            for target in reversed(range(section)):
-                section_copy(
-                    slice_view(weight_in_ref, 0, row),
-                    slice_view(whole, section, row),
-                    slice_send,
-                    slice_recv.at[section],
-                    target,
-                ).start()
-
-    for index in range(RELAYS):
-
-        @pl.when(dp != relay_spot(index))
-        def _(index=index):
-            spread_copy(index).start()
-
-        @pl.when(dp == relay_spot(index))
-        def _(index=index):
-            spread[relay_spot(index)] = moments[index]
 
     def outward(part, carry):
         columns = pl.ds(pl.multiple_of(part * chunk, 128), chunk)
@@ -368,11 +373,12 @@
 
             @pl.when(me < section)
             def _(section=section):
-                took(slice_view(whole, section, row_of(section)), slice_recv.at[section])
+                @pl.when((me >= half) | (me + half != section))
+                def _():
+                    took(slice_view(whole, section, row_of(section)), slice_recv.at[section])
+
                 for shift in (1, 3, 2):
                     wide_copy(section, shift).start()
-
-    spread_adapters([section for section in range(1, sections) if section not in ALONG_Z])
 
     def moved_copy(step):
         peer = lax.rem(dp + step, replicas)
@@ -385,6 +391,17 @@
             device_id_type=MESH,
         )
 
+    for index in range(RELAYS):
+
+        @pl.when(dp != relay_spot(index))
+        def _(index=index):
+            spread_copy(index).start()
+
+        @pl.when(dp == relay_spot(index))
+        def _(index=index):
+            spread[relay_spot(index)] = moments[index]
+
+    spread_adapters([section for section in range(1, sections) if section not in ALONG_Z])
     took(uv_got.at[pl.ds(0, sections - 1)], uv_recv)
     for section in range(1, sections):
 
@@ -419,31 +436,6 @@
             p_copy(section).start()
 
     spread_adapters(ALONG_Z)
-
-    @pl.when(is_relay)
-    def _():
-        took(spread.at[pl.ds(0, replicas - 1)], spread_recv)
-
-        def pick(target, carry):
-            rows = spread[table_ref[0, target]].astype(F32)
-            upper = table_ref[1, target] > 0
-            for which in range(2):
-                start = 2 * which * relay_rows
-                low = rows[start : start + relay_rows]
-                high = rows[start + relay_rows : start + 2 * relay_rows]
-                picked[target, which * relay_rows : (which + 1) * relay_rows, :] = jnp.where(
-                    upper, high, low
-                ).astype(BF)
-            return carry
-
-        lax.fori_loop(0, replicas, pick, 0)
-
-        def moved_start(step, carry):
-            moved_copy(step).start()
-            return carry
-
-        lax.fori_loop(1, replicas, moved_start, 0)
-        moved[relay] = picked[dp]
 
     for section in range(sections):
 
@@ -516,13 +508,13 @@
     for far in order:
         there = lax.rem(z + far, ND)
         for column in range(NY):
-            half_out[far, column] = held[table_ref[2, (other * ND + there) * NY + column]].astype(BF)
+            half_out[far, column] = held[table_ref[(there * NY + column) * NC + other]].astype(BF)
         half_copy(far).start()
     for far in order:
         there = lax.rem(z + far, ND)
         half_copy(far).wait_recv()
         for column in range(NY):
-            own = held[table_ref[2, (core * ND + there) * NY + column]]
+            own = held[table_ref[(there * NY + column) * NC + core]]
             y_out[far, column] = (own + half_got[far, column].astype(F32)).astype(BF)
         for step in (2, 1, 3):
             y_copy(far, step).start()
@@ -541,10 +533,35 @@
 
     place = lax.broadcasted_iota(jnp.int32, (tok_rows, lanes), 1) // rank
     for micro in range(sections):
-        value = p_got[table_ref[3, micro]]
+        value = p_got[plan_ref[micro]]
         left[micro * tok_rows : (micro + 1) * tok_rows, :] = jnp.where(
             place >= me, value, jnp.zeros_like(value)
         )
+
+    @pl.when(is_relay)
+    def _():
+        took(spread.at[pl.ds(0, replicas - 1)], spread_recv)
+
+        def pick(target, carry):
+            rows = spread[old_ref[table_ref[target] // 2]].astype(F32)
+            upper = lax.rem(table_ref[target], 2) > 0
+            for which in range(2):
+                start = 2 * which * relay_rows
+                low = rows[start : start + relay_rows]
+                high = rows[start + relay_rows : start + 2 * relay_rows]
+                picked[target, which * relay_rows : (which + 1) * relay_rows, :] = jnp.where(
+                    upper, high, low
+                ).astype(BF)
+            return carry
+
+        lax.fori_loop(0, replicas, pick, 0)
+
+        def moved_start(step, carry):
+            moved_copy(step).start()
+            return carry
+
+        lax.fori_loop(1, replicas, moved_start, 0)
+        moved[relay] = picked[dp]
 
     for section in range(1, sections):
 
@@ -572,14 +589,8 @@
         def _(section=section):
             pair_copy(section).wait_recv()
 
-    slabs = out_sem.shape[0]
+    slabs = 7
     slab = width // slabs
-
-    def out_copy(index):
-        columns = pl.ds(pl.multiple_of(index * slab, 128), slab)
-        return pltpu.make_async_copy(
-            out.at[:, :, columns], emitted_ref.at[:, :, columns], out_sem.at[index]
-        )
 
     def emit(index, carry):
         columns = pl.ds(pl.multiple_of(index * slab, 128), slab)
@@ -587,9 +598,8 @@
         for micro in range(sections):
             added = result[micro * tok_rows : (micro + 1) * tok_rows]
             out[micro, :, columns] = (
-                base[table_ref[3, micro], :, columns].astype(F32) + added
+                base[plan_ref[micro], :, columns].astype(F32) + added
             ).astype(BF)
-        out_copy(index).start()
         return carry
 
     lax.fori_loop(0, slabs, emit, 0)
@@ -629,22 +639,9 @@
         took(moved, moved_recv)
         sent(spread.at[pl.ds(0, RELAYS)], spread_send)
 
-    is_out = table_ref[4, 0] >= half_blocks
+    is_out = table_ref[dp] >= half_blocks
     main = summed[:block_rows, :]
-    grads = jnp.where(is_out, main + extra_rows[...], main) / loss_scale
-    for index in range(RELAYS):
-        at = slice(index * relay_rows, (index + 1) * relay_rows)
-        old = moved[index].astype(F32)
-        g = grads[at]
-        first_next = beta_one * old[:relay_rows] + (1.0 - beta_one) * g
-        second_next = beta_two * old[relay_rows:] + (1.0 - beta_two) * g * g
-        next_first_ref[at, :] = first_next
-        next_second_ref[at, :] = second_next
-        update_ref[at, :] = (
-            first_next
-            / (1.0 - beta_one**adam_step)
-            / (jnp.sqrt(second_next / (1.0 - beta_two**adam_step)) + adam_eps)
-        )
+    grads_ref[...] = jnp.where(is_out, main + extra_rows[...], main) / loss_scale
 
     @pl.when(me < hop)
     def _():
@@ -654,6 +651,10 @@
     def _():
         sent(prod.at[0, pl.ds(0, replicas - 1)], prod_send)
 
+    @pl.when(me < half)
+    def _():
+        sent(whole.at[pl.ds(0, 3 * tall), pl.ds(0, wide)], pass_send)
+
     sent(uv_out.at[pl.ds(0, sections - 1)], uv_send)
     for section in range(sections):
 
@@ -666,7 +667,8 @@
         @pl.when(me == section)
         def _(section=section):
             sent(prod.at[pl.ds(0, sections - 1), pl.ds(0, 4 * section)], gather_send)
-            sent(whole.at[pl.ds(0, section * tall), pl.ds(0, wide)], slice_send)
+            copies = len(slice_targets(section))
+            sent(whole.at[pl.ds(0, copies * tall), pl.ds(0, wide)], slice_send)
 
         @pl.when(me < section)
         def _(section=section):
@@ -679,9 +681,6 @@
         if far:
             z_copy(far).wait_send()
 
-    for index in range(slabs):
-        out_copy(index).wait()
-
 
 def vmem():
     return pl.BlockSpec(memory_space=pltpu.VMEM)
@@ -695,7 +694,7 @@
     return pl.BlockSpec(memory_space=pl.ANY)
 
 
-def run_drain(table, inputs, base, turned, weight_out, first, second):
+def run_drain(table, old, plan, inputs, base, turned, weight_out, first, second):
     tokens, width = inputs.shape
     rank = turned.shape[0]
     sections = SECTIONS
@@ -710,17 +709,15 @@
     full = (rows + extra, 128)
     per_section = dma((sections,))
     per_z = dma((ND,))
-    row_shape = jax.ShapeDtypeStruct((rows, 128), F32)
     return pl.pallas_call(
         drain_kernel,
         out_shape=(
-            jax.ShapeDtypeStruct((sections, tok_rows, width), BF),
-            row_shape,
-            row_shape,
-            row_shape,
+            pltpu.VMEM((sections, tok_rows, width), BF),
+            jax.ShapeDtypeStruct((rows, 128), F32),
+            jax.ShapeDtypeStruct((RELAYS, 2 * relay_rows, 128), BF),
         ),
-        in_specs=[smem()] + [hbm()] * 2 + [vmem()] * 4,
-        out_specs=(hbm(), vmem(), vmem(), vmem()),
+        in_specs=[smem()] * 3 + [hbm()] * 2 + [vmem()] * 4,
+        out_specs=(vmem(), vmem(), vmem()),
         scratch_shapes=[
             pltpu.VMEM((tokens, width), BF),
             pltpu.VMEM((sections, tok_rows, width), BF),
@@ -736,11 +733,9 @@
             pltpu.VMEM((RELAYS, 4 * relay_rows, 128), BF),
             pltpu.VMEM((replicas, 4 * relay_rows, 128), BF),
             pltpu.VMEM((replicas, 2 * relay_rows, 128), BF),
-            pltpu.VMEM((RELAYS, 2 * relay_rows, 128), BF),
             pltpu.VMEM((lanes, width), BF),
             pltpu.VMEM((sections, tok_rows, lanes), BF),
             pltpu.VMEM((tokens, lanes), BF),
-            pltpu.VMEM((sections, tok_rows, width), BF),
             pltpu.VMEM((width, rank), F32),
             pltpu.VMEM((half_blocks * rows, 128), F32),
             pltpu.VMEM((half_blocks * extra, 128), F32),
@@ -770,6 +765,7 @@
             dma,
             dma,
             per_section,
+            dma,
             per_section,
             per_section,
             per_section,
@@ -780,13 +776,12 @@
             per_z,
             per_z,
             per_z,
-            dma((7,)),
         ],
         compiler_params=pltpu.CompilerParams(
             collective_id=0, has_side_effects=True, vmem_limit_bytes=60 * 2**20
         ),
         name="drain",
-    )(table, inputs, base, turned, weight_out, first, second)
+    )(table, old, plan, inputs, base, turned, weight_out, first, second)
 
 
 def per_device(
@@ -801,7 +796,6 @@
     plan,
 ):
     replicas = lax.axis_size(DP)
-    my_index = lax.axis_index(DP)
     micro_count, tok_rows, width = activations.shape[1:]
     rank = adapter_in.shape[2]
     tokens = micro_count * tok_rows
@@ -812,26 +806,27 @@
     block_rows = block_len // 128
     relay_rows = block_rows // RELAYS
     replica_ids = jnp.arange(replicas, dtype=jnp.int32)
-
-    dest = replica_ids.reshape(ND, NY, NC).transpose(2, 0, 1).reshape(-1)
-    owner_match = owners_new[None, :] == jnp.concatenate([replica_ids, dest, my_index[None]])[:, None]
-    inverse_all = jnp.sum(jnp.where(owner_match, replica_ids[None, :], 0), axis=1)
-    inverse = inverse_all[:replicas]
-    old_match = (inverse // 2)[:, None] == jnp.arange(owners_old.shape[0], dtype=jnp.int32)[None, :]
-    from_row = jnp.sum(jnp.where(old_match, owners_old[None, :], 0), axis=1)
-    padded = jnp.concatenate([plan, jnp.zeros((replicas - micro_count,), jnp.int32)])
-    my_block = jnp.broadcast_to(inverse_all[2 * replicas :], (replicas,))
-    table = jnp.stack(
-        [from_row, inverse % 2, inverse_all[replicas : 2 * replicas], padded, my_block]
-    )
-    emitted, update, first_next, second_next = run_drain(
+    matches = owners_new[None, :] == replica_ids[:, None]
+    table = jnp.sum(jnp.where(matches, replica_ids[None, :], 0), axis=1)
+    emitted, grads, moved = run_drain(
         table.astype(jnp.int32),
+        owners_old,
+        plan,
         inputs,
         loss_grads,
         adapter_in[0].T,
         adapter_out[0],
         first_moment.reshape(2, RELAYS, relay_rows, 128),
         second_moment.reshape(2, RELAYS, relay_rows, 128),
+    )
+    first_old = moved[:, :relay_rows].astype(F32).reshape(block_rows, 128)
+    second_old = moved[:, relay_rows:].astype(F32).reshape(block_rows, 128)
+    first_next = beta_one * first_old + (1.0 - beta_one) * grads
+    second_next = beta_two * second_old + (1.0 - beta_two) * grads * grads
+    update = (
+        first_next
+        / (1.0 - beta_one**adam_step)
+        / (jnp.sqrt(second_next / (1.0 - beta_two**adam_step)) + adam_eps)
     )
     shape = (1, 1, block_len)
     return (

time: 86.3 us -> 67 us (0.78)
  the two profiles are of different devices: /device:TPU:17 before, /device:TPU:6 now
where the time goes in v3:
time: 67 us; the launch traced here: 66.2 us
  Pallas kernels  61.6 us (92%)
  other arithmetic  2.01 us (3%)
  local copies, waits for them, and re-layouts  2 us (3%)
  between operations  0.67 us (1%)
    pallas_call x1, Pallas kernels, run_drain(): pl.pallas_call(drain_kernel, out_shape=(pltpu.VMEM((sections, tok_rows, w...  61.6 us
    unnamed x5, local copies, waits for them, and re-layouts  2 us

profile of v3, /device:TPU:6, one launch (start us, length us, event | category | flops | bytes accessed | tf_op | source)
XLA Modules:
  0.0 66.2 jit_solution(15719631680427180233)
XLA Ops:
  0.6 1.3 %select_reduce_fusion.table_ref = s32[32]{0:T(128)} fusion(s32[32]{0:T(128)} %bitcast.29), kind=kLoop, calls=%fused_computation.6 | loop fusion | flops 3040 | bytes 256 | tf_op jit(solution)/shard_map/reduce_sum | solution.py:810
  1.9 61.6 %drain.1 = (bf16[8,48,5376]{2,1,0:T(8,128)(2,1)S(1)}, f32[168,128]{1,0:T(8,128)}, bf16[7,48,128]{2,1,0:T(8,128)(2,1)}) custom-call(s32[32]{0:T(128)} %select_reduce_fusion.table_ref, s32[16]{0:T(128)} %bitcast.28, s32[8]{0:T(128)} %plan_ref.1, bf16[384,5376]{1,0:T(8,128)(2,1)} %bitcast.20, bf16[8,48,5376]{2,1,0:T(8,128)(2,1)} %base_ref.1, ...), custom_call_target="tpu_custom_call" | custom-call | tf_op jit(solution)/shard_map/drain/pallas_call | solution.py:712
  63.5 0.0 copy-start
  63.5 0.0 copy-start.1
  63.5 2.0 %copy.14 = bf16[1,8,48,5376]{3,2,1,0:T(8,128)(2,1)} copy(bf16[1,8,48,5376]{3,2,1,0:T(8,128)(2,1)S(1)} %bitcast.19) | data formatting | bytes 8257536
  65.5 0.0 copy-done
  65.5 0.0 copy-done.1
  65.5 0.7 %add_divide_fusion = (f32[168,128]{1,0:T(8,128)}, f32[168,128]{1,0:T(8,128)}, f32[168,128]{1,0:T(8,128)}) fusion(f32[168,128]{1,0:T(8,128)S(1)} %copy-done.1, f32[7,24,128]{2,1,0:T(8,128)S(1)} %get-tuple-element.14, f32[7,24,128]{2,1,0:T(8,128)S(1)} %get-tuple-element.13), kind=kLoop, calls=%fused_computation.3 | loop fusion | flops 150528 | bytes 516096 | tf_op jit(solution)/shard_map/div | solution.py:827
  (1 shorter events, 0.0 us)
Async XLA Ops:
  63.5 2.0 %copy-start = (bf16[7,48,128]{2,1,0:T(8,128)(2,1)S(1)}, bf16[7,48,128]{2,1,0:T(8,128)(2,1)}, u32[]{:S(2)}) copy-start(bf16[7,48,128]{2,1,0:T(8,128)(2,1)} %get-tuple-element.8) | copy-start | bytes 258052
  63.5 2.0 %copy-start.1 = (f32[168,128]{1,0:T(8,128)S(1)}, f32[168,128]{1,0:T(8,128)}, u32[]{:S(2)}) copy-start(f32[168,128]{1,0:T(8,128)} %get-tuple-element.9) | copy-start | bytes 258052
